TPU v7x, 32 devices: a whole 2x2x4 slice. The times are simulated.
32 devices in a mesh: col: 8 (over y, x, core), row: 4 (over z).
Axes of the slice: x: 2, y: 2, z: 4, core: 2. Of those that a mesh axis runs over, the one named last changes fastest.
Arguments:
- rhs: float32 [2, 32, 4, 4096], P(None, None, 'row', 'col'), may hold values from -6 to 6
- u_factor: bfloat16 [64, 40, 2, 256, 128], P('row', 'col'), may hold values from -0.078125 to 0.078125
- v_factor: bfloat16 [64, 40, 2, 256, 128], P('row', 'col'), may hold values from -0.375 to 0.375
- ranks: int32 [64, 40], P('row', 'col'), may hold values from 8 to 128, as said below
- assign: int32 [40], replicated, may hold values from 0 to 39, each once
Outputs:
- solution: float32 [2, 32, 10240], P(None, None, 'col')
- residual_estimate: float32 [32], replicated
Inputs may be any that keep to these rules, and one draw needn't show every extreme that they name: `ranks`: every entry is 128 // 16 times a power of two from 1 to 16.
All inputs are finite; a program needn't handle non-finite values.
Results may differ from a plain program's by a relative error of at most 0.0068.
Values may be sent and summed in bfloat16 or wider, within the bound.
No kernel may reach another device: no remote copies, remote signals or barrier semaphores. Data moves between devices by JAX's collectives and lax.ppermute only.
A program may use at most 128 MiB of HBM per device.

v0:
```python
import jax
import jax.numpy as jnp
from jax import lax
from jax.sharding import PartitionSpec as P

ITERS = 2


def sum_squares(value):
    return jnp.sum(value * value, axis=(0, 2))


def on_device(rhs, u_factor, v_factor, ranks, assign):
    tile_rows = u_factor.shape[0]
    tile_cols = u_factor.shape[1]
    tile_size = u_factor.shape[3]
    rank_cap = u_factor.shape[4]
    sources = rhs.shape[1]
    rank_iota = lax.broadcasted_iota(jnp.int32, (tile_rows, tile_cols, 1, 1, rank_cap), 4)
    mask = (rank_iota < ranks[:, :, None, None, None]).astype(jnp.float32)

    def adjoint_terms(group_data):
        data_b = group_data.reshape(2, sources, tile_rows, tile_size)
        raw = jnp.einsum("ipcnk,dsin->ipcdsk", u_factor, data_b, preferred_element_type=jnp.float32)
        coeff = jnp.stack(
            [raw[:, :, 0, 0] + raw[:, :, 1, 1], raw[:, :, 0, 1] - raw[:, :, 1, 0]], axis=2
        )
        coeff = (coeff * mask).astype(jnp.bfloat16)
        prod = jnp.einsum("ipcnk,ipdsk->cdspn", v_factor, coeff, preferred_element_type=jnp.float32)
        partial_model = jnp.stack([prod[0, 0] + prod[1, 1], prod[0, 1] - prod[1, 0]], axis=0)
        return partial_model.reshape(2, sources, tile_cols * tile_size)

    def adjoint_step(data_hat, v_prev):
        group_data = lax.all_gather(data_hat.astype(jnp.bfloat16), "col", axis=2, tiled=True)
        beta_now = jnp.sqrt(lax.psum(sum_squares(data_hat), ("col", "row")))
        model_sum = lax.psum(adjoint_terms(group_data), "row")
        v_hat = model_sum / beta_now[None, :, None] - beta_now[None, :, None] * v_prev
        alpha_now = jnp.sqrt(lax.psum(sum_squares(v_hat), "col"))
        return (
            data_hat / beta_now[None, :, None],
            beta_now,
            v_hat / alpha_now[None, :, None],
            alpha_now,
        )

    data_first = rhs.reshape(2, sources, rhs.shape[3])
    zero_model = jnp.zeros((2, sources, tile_cols * tile_size), jnp.float32)
    u_vec, beta_now, v_vec, alpha_now = adjoint_step(data_first, zero_model)
    w_vec = v_vec
    x_vec = zero_model
    phibar = beta_now
    rhobar = alpha_now
    for iteration in range(ITERS):
        model_b = v_vec.astype(jnp.bfloat16).reshape(2, sources, tile_cols, tile_size)
        forward_raw = jnp.einsum(
            "ipcnk,dspn->ipcdsk", v_factor, model_b, preferred_element_type=jnp.float32
        )
        forward_coeff = jnp.stack(
            [
                forward_raw[:, :, 0, 0] - forward_raw[:, :, 1, 1],
                forward_raw[:, :, 0, 1] + forward_raw[:, :, 1, 0],
            ],
            axis=2,
        )
        forward_coeff = (forward_coeff * mask).astype(jnp.bfloat16)
        forward_prod = jnp.einsum(
            "ipcnk,ipdsk->cdsin", u_factor, forward_coeff, preferred_element_type=jnp.float32
        )
        partial_data = jnp.stack(
            [forward_prod[0, 0] - forward_prod[1, 1], forward_prod[0, 1] + forward_prod[1, 0]],
            axis=0,
        )
        partial_data = partial_data.reshape(2, sources, tile_rows * tile_size)
        data_hat = (
            lax.psum_scatter(partial_data, "col", scatter_dimension=2, tiled=True)
            - alpha_now[None, :, None] * u_vec
        )
        u_vec, beta_now, v_vec, alpha_now = adjoint_step(data_hat, v_vec)
        rho_now = jnp.sqrt(rhobar * rhobar + beta_now * beta_now)
        cosine = rhobar / rho_now
        sine = beta_now / rho_now
        theta = sine * alpha_now
        rhobar = -cosine * alpha_now
        phi_now = cosine * phibar
        phibar = sine * phibar
        x_vec = x_vec + (phi_now / rho_now)[None, :, None] * w_vec
        w_vec = v_vec - (theta / rho_now)[None, :, None] * w_vec
    all_cols = assign.shape[0]
    natural = lax.axis_index("col") * tile_cols + jnp.arange(tile_cols, dtype=jnp.int32)
    positions = jnp.arange(all_cols, dtype=jnp.int32)
    where_held = jnp.sum(
        positions[None, :] * (assign[None, :] == natural[:, None]).astype(jnp.int32), axis=1
    )
    share = sources // lax.axis_size("row")
    own_share = lax.dynamic_slice_in_dim(x_vec, lax.axis_index("row") * share, share, 1)
    gathered = lax.all_gather(own_share, "col", axis=2, tiled=True)
    gathered = gathered.reshape(2, share, all_cols, tile_size)
    picked = jnp.take(gathered, where_held, axis=2).reshape(2, share, tile_cols * tile_size)
    solution = lax.all_gather(picked, "row", axis=1, tiled=True)
    return (solution, phibar)


def solution(mesh):
    in_specs = (
        P(None, None, "row", "col"),
        P("row", "col", None, None, None),
        P("row", "col", None, None, None),
        P("row", "col"),
        P(),
    )
    out_specs = (P(None, None, "col"), P())
    return jax.shard_map(
        on_device, mesh=mesh, in_specs=in_specs, out_specs=out_specs, check_vma=False
    )
```

profile of v0, /device:TPU:0, one launch (start us, length us, event | category | flops | bytes accessed | tf_op | source)
XLA Modules:
  0.0 338.9 jit_solution(15961958501180942365)
XLA Ops:
  8.1 11.3 %all_gather.12 = bf16[2,32,4096]{2,1,0:T(8,128)(2,1)S(1)} all-gather(bf16[2,32,512]{2,1,0:T(8,128)(2,1)S(1)} %bitcast.164), channel_id=1, replica_groups=mesh['col'=8,'row'=4] {'col'}, dimensions={2}, use_global_device_ids=true | all-gather | bytes 589824 | tf_op jit(solution)/shard_map/all_gather | solution.py:34
  19.6 6.1 %fusion.29 = f32[16,5,2,2,32,128]{5,4,2,1,3,0:T(8,128)S(1)} fusion(bf16[16,5,2,256,128]{4,3,2,1,0:T(8,128)(2,1)} %param.6, bf16[2,32,16,256,1,1]{3,2,1,0,5,4:T(8,128)(2,1)S(1)} %bitcast_bitcast_fusion.1), kind=kOutput, calls=%fused_computation.28 | convolution fusion | flops 671088640 | bytes 16252928 | tf_op jit(solution)/shard_map/ipcnk,dsin->ipcdsk/dot_general | solution.py:24
  26.8 5.9 %fusion.55 = f32[2,2,32,5,256]{4,2,0,1,3:T(8,128)S(1)} fusion(bf16[16,5,2,256,128]{4,3,2,1,0:T(8,128)(2,1)} %param.7, f32[16,5,1,32,128]{4,3,1,0,2:T(8,128)S(1)} %fusion.48, f32[16,5,1,32,128]{4,3,1,0,2:T(8,128)S(1)} %fusion.50, f32[16,5,128]{2,1,0:T(8,128)S(1)} %fusion.74), kind=kOutput, calls=%fused_computation.57 | convolution fusion | flops 673054720 | bytes 13803520 | tf_op jit(solution)/shard_map/ipcnk,ipdsk->cdspn/dot_general | solution.py:29
  34.1 39.7 %psum.50 = f32[32]{0:T(128)S(1)} all-reduce(f32[32]{0:T(128)S(1)} %fusion.69), channel_id=1, replica_groups=mesh['col'=8,'row'=4] {'col','row'}, use_global_device_ids=true, to_apply=%region_3.0 | all-reduce | flops 32 | bytes 256 | tf_op jit(solution)/shard_map/psum | solution.py:35
  73.9 1.2 multiply_reduce_fusion.1
  75.1 12.7 %psum.51 = f32[32]{0:T(128)S(1)} all-reduce(f32[32]{0:T(128)S(1)} %multiply_reduce_fusion.1), channel_id=1, replica_groups=mesh['col'=8,'row'=4] {'col'}, use_global_device_ids=true, to_apply=%region_5.0 | all-reduce | flops 32 | bytes 256 | tf_op jit(solution)/shard_map/psum | solution.py:38
  87.8 1.2 fusion.78
  89.2 5.2 %fusion.20 = f32[16,5,2,2,32,128]{5,4,1,0,3,2:T(8,128)S(1)} fusion(bf16[2,32,5,256,1,1]{3,2,1,0,5,4:T(8,128)(2,1)S(1)} %bitcast.160, bf16[16,5,2,256,128]{4,3,2,1,0:T(8,128)(2,1)} %param.7), kind=kOutput, calls=%fused_computation.25 | convolution fusion | flops 671088640 | bytes 15892480 | tf_op jit(solution)/shard_map/ipcnk,dspn->ipcdsk/dot_general | solution.py:55
  94.5 1.7 fusion.47
  96.2 4.6 %fusion.32 = f32[2,2,32,16,256]{4,2,0,1,3:T(8,128)S(1)} fusion(bf16[16,5,2,256,128]{4,3,2,1,0:T(8,128)(2,1)S(1)} %bitcast.150, f32[16,5,1,32,128]{4,3,1,0,2:T(8,128)} %get-tuple-element.17, f32[16,5,1,32,128]{4,3,1,0,2:T(8,128)S(1)} %get-tuple-element.16, f32[16,5,128]{2,1,0:T(8,128)S(1)} %fusion.74), kind=kOutput, calls=%fused_computation.29 | convolution fusion | flops 673054720 | bytes 15245312 | tf_op jit(solution)/shard_map/ipcnk,ipdsk->cdsin/dot_general | solution.py:66
  102.9 35.1 %reduce-scatter.3.cloned.1.call-done = f32[2,32,512]{2,1,0:T(8,128)} async-done(((f32[2,32,4096]{2,1,0:T(8,128)}), f32[2,32,512]{2,1,0:T(8,128)}) %reduce-scatter.3.cloned.1.call-update) | async-done | bytes 131088 | tf_op jit(solution)/shard_map/reduce_scatter | solution.py:75
  139.1 10.0 %all_gather.13 = bf16[2,32,4096]{2,1,0:T(8,128)(2,1)S(1)} all-gather(bf16[2,32,512]{2,1,0:T(8,128)(2,1)S(1)} %convert_element_type.38), channel_id=1, replica_groups=mesh['col'=8,'row'=4] {'col'}, dimensions={2}, use_global_device_ids=true | all-gather | bytes 589824 | tf_op jit(solution)/shard_map/all_gather | solution.py:34
  149.3 5.2 %fusion.26 = f32[16,5,2,2,32,128]{5,4,1,0,3,2:T(8,128)S(1)} fusion(bf16[2,32,16,256,1,1]{3,2,1,0,5,4:T(8,128)(2,1)S(1)} %bitcast_bitcast_fusion, bf16[16,5,2,256,128]{4,3,2,1,0:T(8,128)(2,1)} %param.6), kind=kOutput, calls=%fused_computation.27 | convolution fusion | flops 671088640 | bytes 16252928 | tf_op jit(solution)/shard_map/ipcnk,dsin->ipcdsk/dot_general | solution.py:24
  156.3 3.3 fusion.60
  160.8 39.6 %psum.52 = f32[32]{0:T(128)S(1)} all-reduce(f32[32]{0:T(128)S(1)} %get-tuple-element.8), channel_id=1, replica_groups=mesh['col'=8,'row'=4] {'col','row'}, use_global_device_ids=true, to_apply=%region_8.0 | all-reduce | flops 32 | bytes 256 | tf_op jit(solution)/shard_map/psum | solution.py:35
  200.4 1.4 multiply_reduce_fusion
  201.7 12.7 %psum.54 = f32[32]{0:T(128)S(1)} all-reduce(f32[32]{0:T(128)S(1)} %multiply_reduce_fusion), channel_id=1, replica_groups=mesh['col'=8,'row'=4] {'col'}, use_global_device_ids=true, to_apply=%region_11.0 | all-reduce | flops 32 | bytes 256 | tf_op jit(solution)/shard_map/psum | solution.py:38
  215.8 5.2 %fusion.23 = f32[16,5,2,2,32,128]{5,4,1,0,3,2:T(8,128)S(1)} fusion(bf16[2,32,5,256,1,1]{3,2,1,0,5,4:T(8,128)(2,1)S(1)} %bitcast.161, bf16[16,5,2,256,128]{4,3,2,1,0:T(8,128)(2,1)} %param.7), kind=kOutput, calls=%fused_computation.26 | convolution fusion | flops 671088640 | bytes 15892480 | tf_op jit(solution)/shard_map/ipcnk,dspn->ipcdsk/dot_general | solution.py:55
  221.0 1.7 fusion.43
  222.7 4.6 %fusion.35 = f32[2,2,32,16,256]{4,2,0,1,3:T(8,128)S(1)} fusion(bf16[16,5,2,256,128]{4,3,2,1,0:T(8,128)(2,1)S(1)} %bitcast.152, f32[16,5,1,32,128]{4,3,1,0,2:T(8,128)} %get-tuple-element.13, f32[16,5,1,32,128]{4,3,1,0,2:T(8,128)S(1)} %get-tuple-element.12, f32[16,5,128]{2,1,0:T(8,128)S(1)} %fusion.74), kind=kOutput, calls=%fused_computation.30 | convolution fusion | flops 673054720 | bytes 15245312 | tf_op jit(solution)/shard_map/ipcnk,ipdsk->cdsin/dot_general | solution.py:66
  229.7 34.9 %reduce-scatter.5.cloned.1.call-done = f32[2,32,512]{2,1,0:T(8,128)} async-done(((f32[2,32,4096]{2,1,0:T(8,128)}), f32[2,32,512]{2,1,0:T(8,128)}) %reduce-scatter.5.cloned.1.call-update) | async-done | bytes 131088 | tf_op jit(solution)/shard_map/reduce_scatter | solution.py:75
  265.7 39.3 %psum.55 = f32[32]{0:T(128)S(1)} all-reduce(f32[32]{0:T(128)S(1)} %multiply_reduce_fusion.2), channel_id=1, replica_groups=mesh['col'=8,'row'=4] {'col','row'}, use_global_device_ids=true, to_apply=%region_14.0 | all-reduce | flops 32 | bytes 256 | tf_op jit(solution)/shard_map/psum | solution.py:35
  305.9 10.9 %all_gather.14 = f32[2,8,10240]{2,1,0:T(8,128)S(1)} all-gather(f32[2,8,1280]{2,1,0:T(8,128)S(1)} %fusion.73), channel_id=1, replica_groups=mesh['col'=8,'row'=4] {'col'}, dimensions={2}, use_global_device_ids=true | all-gather | bytes 737280 | tf_op jit(solution)/shard_map/all_gather | solution.py:96
  317.4 14.3 %all_gather.15 = f32[2,32,1280]{2,1,0:T(8,128)S(1)} all-gather(f32[2,8,1280]{2,1,0:T(8,128)S(1)} %broadcast_select_fusion), channel_id=1, replica_groups=mesh['col'=8,'row'=4] {'row'}, dimensions={1}, use_global_device_ids=true | all-gather | bytes 409600 | tf_op jit(solution)/shard_map/all_gather | solution.py:99
  (99 shorter events, 17.0 us)
Async XLA Ops:
  7.2 66.7 %all-reduce.3.cloned.1.call-start = ((), (), s32[]{:S(2)}) async-start(), calls=%async_computation.2 | async-start | bytes 655360 | tf_op jit(solution)/shard_map/psum | solution.py:36
  26.0 0.7 copy-start.1
  32.7 1.3 copy-start
  33.9 104.1 %reduce-scatter.3.cloned.1.call-start = ((), (), s32[]{:S(2)}) async-start(), calls=%async_computation.3 | async-start | bytes 1179648 | tf_op jit(solution)/shard_map/reduce_scatter | solution.py:75
  87.8 8.4 %slice-start = ((s8[10485760]{0:T(1024)(128)(4,1)}), s8[2097152]{0:T(1024)(128)(4,1)S(1)}, s32[]{:S(2)}) async-start(s8[10485760]{0:T(1024)(128)(4,1)} %bitcast.149), calls=%async_computation.6 | async-start | bytes 4194304
  89.2 6.9 %slice-start.1 = ((s8[10485760]{0:T(1024)(128)(4,1)}), s8[4194304]{0:T(1024)(128)(4,1)S(1)}, s32[]{:S(2)}) async-start(s8[10485760]{0:T(1024)(128)(4,1)} %bitcast.149), calls=%async_computation.7 | async-start | bytes 8388608
  89.2 6.9 %slice-start.2 = ((s8[10485760]{0:T(1024)(128)(4,1)}), s8[4194304]{0:T(1024)(128)(4,1)S(1)}, s32[]{:S(2)}) async-start(s8[10485760]{0:T(1024)(128)(4,1)} %bitcast.149), calls=%async_computation.8 | async-start | bytes 8388608
  102.8 97.5 %all-reduce.5.cloned.1.call-start = ((), (), s32[]{:S(2)}) async-start(), calls=%async_computation.4 | async-start | bytes 655360 | tf_op jit(solution)/shard_map/psum | solution.py:36
  149.1 6.0 %slice-start.6 = ((s8[10485760]{0:T(1024)(128)(4,1)}), s8[4194304]{0:T(1024)(128)(4,1)S(1)}, s32[]{:S(2)}) async-start(s8[10485760]{0:T(1024)(128)(4,1)} %bitcast.153), calls=%async_computation.12 | async-start | bytes 8388608
  149.3 6.4 %slice-start.7 = ((s8[10485760]{0:T(1024)(128)(4,1)}), s8[4194304]{0:T(1024)(128)(4,1)S(1)}, s32[]{:S(2)}) async-start(s8[10485760]{0:T(1024)(128)(4,1)} %bitcast.153), calls=%async_computation.13 | async-start | bytes 8388608
  149.3 7.0 %slice-start.8 = ((s8[10485760]{0:T(1024)(128)(4,1)}), s8[2097152]{0:T(1024)(128)(4,1)S(1)}, s32[]{:S(2)}) async-start(s8[10485760]{0:T(1024)(128)(4,1)} %bitcast.153), calls=%async_computation.14 | async-start | bytes 4194304
  160.7 103.9 %reduce-scatter.5.cloned.1.call-start = ((), (), s32[]{:S(2)}) async-start(), calls=%async_computation.5 | async-start | bytes 1179648 | tf_op jit(solution)/shard_map/reduce_scatter | solution.py:75
  200.4 22.3 %slice-start.3 = ((s8[10485760]{0:T(1024)(128)(4,1)}), s8[2097152]{0:T(1024)(128)(4,1)S(1)}, s32[]{:S(2)}) async-start(s8[10485760]{0:T(1024)(128)(4,1)} %bitcast.151), calls=%async_computation.9 | async-start | bytes 4194304
  215.7 6.9 %slice-start.4 = ((s8[10485760]{0:T(1024)(128)(4,1)}), s8[4194304]{0:T(1024)(128)(4,1)S(1)}, s32[]{:S(2)}) async-start(s8[10485760]{0:T(1024)(128)(4,1)} %bitcast.151), calls=%async_computation.10 | async-start | bytes 8388608
  215.7 6.9 %slice-start.5 = ((s8[10485760]{0:T(1024)(128)(4,1)}), s8[4194304]{0:T(1024)(128)(4,1)S(1)}, s32[]{:S(2)}) async-start(s8[10485760]{0:T(1024)(128)(4,1)} %bitcast.151), calls=%async_computation.11 | async-start | bytes 8388608
  227.9 1.5 copy-start.2
Sparse Core Ops, SparseCore 0:
  34.0 36.6 all-reduce.2
  103.0 34.9 reduce-scatter.2
  160.8 36.2 all-reduce.4
  229.5 35.0 reduce-scatter.4
where the time goes:
time: 340 us; the launch traced here: 339 us
  blocking collectives  190 us (56%)
  waiting for transfers between devices  70.1 us (21%)
  matrix products  40 us (12%)
  other arithmetic  16.8 us (5%)
  between operations  14.3 us (4%)
  local copies, waits for them, and re-layouts  7.14 us (2%)
    psum x3, blocking collectives, adjoint_step(): beta_now = jnp.sqrt(lax.psum(sum_squares(data_hat), ('col', 'row')))  119 us
    reduce_scatter x2, waiting for transfers between devices, on_device(): lax.psum_scatter(partial_data, 'col', scatter_dimension=2, tiled=True)  70 us
    psum x2, blocking collectives, adjoint_step(): alpha_now = jnp.sqrt(lax.psum(sum_squares(v_hat), 'col'))  25.4 us
    all_gather x2, blocking collectives, adjoint_step(): lax.all_gather(data_hat.astype(jnp.bfloat16), 'col', axis=2, tiled=True)  21.3 us
    all_gather x1, blocking collectives, on_device(): solution = lax.all_gather(picked, 'row', axis=1, tiled=True)  14.3 us
    dot_general x2, matrix products, adjoint_terms(): jnp.einsum('ipcnk,dsin->ipcdsk', u_factor, data_b, preferred_element_type...  11.3 us
    all_gather x1, blocking collectives, on_device(): gathered = lax.all_gather(own_share, 'col', axis=2, tiled=True)  10.9 us
    dot_general x2, matrix products, on_device(): jnp.einsum('ipcnk,dspn->ipcdsk', v_factor, model_b, preferred_element_typ...  10.4 us
  transfers between devices with their start and end apart: 4, of which 2 were waited for; matrix products, arithmetic and copies ran while one was open for 0% of the time, Pallas kernels for 0%

commit v1 on v0

v1 whole, which is shorter than its diff:
```python
import functools

import jax
import jax.numpy as jnp
from jax import lax
from jax.experimental import pallas as pl
from jax.experimental.pallas import tpu as pltpu
from jax.sharding import PartitionSpec as P

F32 = jnp.float32
BF16 = jnp.bfloat16
EXT = 128
VMEM = pl.BlockSpec(memory_space=pltpu.VMEM)
SMEM = pl.BlockSpec(memory_space=pltpu.SMEM)
PARAMS = pltpu.CompilerParams(vmem_limit_bytes=48 * 1024 * 1024)


def lanes_of(columns, rows):
    lane = lax.broadcasted_iota(jnp.int32, (rows, EXT), 1)
    out = jnp.zeros((rows, EXT), F32)
    for number, column in enumerate(columns):
        rest = column
        for term in range(3):
            part = rest.astype(BF16).astype(F32)
            rest = rest - part
            out = jnp.where(lane == 3 * number + term, part, out)
    return out.astype(BF16)


def column_of(ext, number):
    lane = lax.broadcasted_iota(jnp.int32, ext.shape, 1)
    chosen = (lane >= 3 * number) & (lane < 3 * number + 3)
    return jnp.sum(jnp.where(chosen, ext, 0.0), axis=1, keepdims=True)


def both_parts(column, half):
    real, imag = parts_of(column, half)
    return join(real + imag, real + imag)


def parts_of(raw, half):
    rows, width = raw.shape
    split = raw.reshape(rows // (2 * half), 2, half, width)
    return split[:, 0], split[:, 1]


def join(first, second):
    groups, half, width = first.shape
    return jnp.stack([first, second], axis=1).reshape(groups * 2 * half, width)


def tile_coeff(vec, tile, rank, conj, half):
    k = tile.shape[2]
    raw = jnp.dot(vec, jnp.concatenate([tile[0], tile[1]], axis=1), preferred_element_type=F32)
    rr, ri = parts_of(raw[:, :k], half)
    ir, ii = parts_of(raw[:, k:], half)
    if conj:
        real, imag = rr + ii, ri - ir
    else:
        real, imag = rr - ii, ri + ir
    lane = lax.broadcasted_iota(jnp.int32, real.shape, 2)
    real = jnp.where(lane < rank, real, 0.0)
    imag = jnp.where(lane < rank, imag, 0.0)
    if conj:
        left = jnp.concatenate([join(real, imag), join(imag, -real)], axis=1)
    else:
        left = jnp.concatenate([join(real, imag), join(-imag, real)], axis=1)
    return left.astype(BF16)


def expand(left, tile):
    right = jnp.concatenate([tile[0], tile[1]], axis=1)
    return lax.dot_general(left, right, (((1,), (1,)), ((), ())), preferred_element_type=F32)


def adjoint_body(n_col, n_row, place, ranks, u_ref, v_ref, *refs):
    pieces, outs, (d_scr, z_scr) = refs[:n_col], refs[n_col : n_col + n_row], refs[n_col + n_row :]
    step = pl.program_id(0)
    tile_cols, tile_size = u_ref.shape[1], u_ref.shape[3]
    local = pieces[0].shape[1] - EXT

    @pl.when(step == 0)
    def _():
        z_scr[...] = jnp.zeros_like(z_scr)
        for j, piece in enumerate(pieces):
            held = jnp.bitwise_xor(place[0], j)
            if local >= tile_size:
                for w in range(local // tile_size):
                    d_scr[held * (local // tile_size) + w] = piece[:, w * tile_size : (w + 1) * tile_size]
            else:
                share = tile_size // local
                d_scr[held // share, :, pl.ds(pl.multiple_of((held % share) * local, local), local)] = piece[:, :local]

    data = d_scr[step]
    for p in range(tile_cols):
        left = tile_coeff(data, u_ref[0, p], ranks[step, p], True, data.shape[0] // (2 * n_row))
        z_scr[:, p * tile_size : (p + 1) * tile_size] += expand(left, v_ref[0, p])

    @pl.when(step == pl.num_programs(0) - 1)
    def _():
        width = tile_cols * tile_size
        ext = sum(piece[:, local:].astype(F32) for piece in pieces)
        ext = lanes_of([column_of(ext, 0)], ext.shape[0])
        for k, out in enumerate(outs):
            rows = out.shape[0]
            out[:, :width] = z_scr[k * rows : (k + 1) * rows, :].astype(BF16)
            out[:, width:] = ext[k * rows : (k + 1) * rows, :]


def forward_body(n_col, n_row, place, ranks, u_ref, v_ref, *refs):
    pieces, outs, (x_scr, y_scr) = refs[:n_row], refs[n_row : n_row + n_col], refs[n_row + n_col :]
    step = pl.program_id(0)
    tile_cols, tile_size = u_ref.shape[1], u_ref.shape[3]
    width = tile_cols * tile_size

    @pl.when(step == 0)
    def _():
        for k, piece in enumerate(pieces):
            rows = piece.shape[0]
            x_scr[k * rows : (k + 1) * rows, :] = piece[...]

    total = None
    for p in range(tile_cols):
        model = x_scr[:, p * tile_size : (p + 1) * tile_size]
        left = tile_coeff(model, v_ref[0, p], ranks[step, p], False, model.shape[0] // (2 * n_row))
        term = expand(left, u_ref[0, p])
        total = term if total is None else total + term
    y_scr[step] = total.astype(BF16)

    @pl.when(step == pl.num_programs(0) - 1)
    def _():
        for j, out in enumerate(outs):
            local = out.shape[1] - EXT
            held = jnp.bitwise_xor(place[0], j)
            if local >= tile_size:
                for w in range(local // tile_size):
                    out[:, w * tile_size : (w + 1) * tile_size] = y_scr[held * (local // tile_size) + w]
            else:
                share = tile_size // local
                out[:, :local] = y_scr[held // share, :, pl.ds(pl.multiple_of((held % share) * local, local), local)]
            out[:, local:] = x_scr[:, width:]


def product(body, place, ranks, u_factor, v_factor, pieces, out_shapes, scratch):
    tile_rows, tile_cols, _, tile_size, rank_cap = u_factor.shape
    block = pl.BlockSpec((1, tile_cols, 2, tile_size, rank_cap), lambda i, *_: (i, 0, 0, 0, 0))
    whole = lambda shape: pl.BlockSpec(shape, lambda i, *_: (0,) * len(shape))
    return pl.pallas_call(
        body,
        grid_spec=pltpu.PrefetchScalarGridSpec(
            num_scalar_prefetch=2,
            grid=(tile_rows,),
            in_specs=[block, block] + [whole(piece.shape) for piece in pieces],
            out_specs=[whole(shape.shape) for shape in out_shapes],
            scratch_shapes=scratch,
        ),
        out_shape=out_shapes,
        compiler_params=PARAMS,
    )(place, ranks, u_factor, v_factor, *pieces)


def small(body, out_shapes, *args):
    return pl.pallas_call(
        body,
        in_specs=[SMEM if arg.dtype == jnp.int32 else VMEM for arg in args],
        out_specs=[VMEM] * len(out_shapes),
        out_shape=out_shapes,
        compiler_params=PARAMS,
    )(*args)


def total_of(refs, rows, columns):
    return sum(ref[rows, columns].astype(F32) for ref in refs)


def begin_body(n_row, place, rhs, data, payload):
    rows, local = data.shape
    half = rows // (2 * n_row)
    for k in range(n_row):
        held = jnp.bitwise_xor(place[1], k)
        for part in range(2):
            at = (2 * k + part) * half
            data[at : at + half, :] = rhs[part, pl.ds(pl.multiple_of(held * half, half), half), :]
    values = data[...]
    payload[:, :local] = values.astype(BF16)
    payload[:, local:] = lanes_of([jnp.sum(values * values, axis=1, keepdims=True)], rows)


def model_first_body(n_row, *refs):
    pieces, (v_hat, payload) = refs[:n_row], refs[n_row:]
    width = v_hat.shape[1]
    total = total_of(pieces, slice(None), slice(0, width))
    beta2 = both_parts(column_of(total_of(pieces, slice(None), slice(width, None)), 0), total.shape[0] // 2)
    value = total / jnp.sqrt(beta2)
    v_hat[...] = value
    payload[:, :width] = value.astype(BF16)
    payload[:, width:] = lanes_of([beta2, jnp.sum(value * value, axis=1, keepdims=True)], value.shape[0])


def model_next_body(n_row, v_prev, scalars, *refs):
    pieces, (payload,) = refs[:n_row], refs[n_row:]
    rows, width = v_prev.shape
    total = total_of(pieces, slice(None), slice(0, width))
    beta2 = both_parts(column_of(total_of(pieces, slice(None), slice(width, None)), 0), total.shape[0] // 2)
    beta = jnp.sqrt(beta2)
    alpha_prev = scalars[:rows, 0:1]
    value = total / beta - (beta / alpha_prev) * v_prev[...]
    payload[:, :width] = value.astype(BF16)
    payload[:, width:] = lanes_of([beta2, jnp.sum(value * value, axis=1, keepdims=True)], rows)


def scalars_of(pieces, local, n_col, n_row):
    ext = total_of(pieces, slice(None), slice(local, None))
    beta = jnp.sqrt(column_of(ext, 0) * (1.0 / n_col))
    alpha = jnp.sqrt(both_parts(column_of(ext, 1), ext.shape[0] // (2 * n_row)))
    return alpha, beta


def data_next_body(n_col, n_row, data_prev, *refs):
    pieces, (data, payload, scalars) = refs[:n_col], refs[n_col:]
    rows, local = data_prev.shape
    alpha, beta = scalars_of(pieces, local, n_col, n_row)
    value = total_of(pieces, slice(None), slice(0, local)) / alpha - (alpha / beta) * data_prev[...]
    data[...] = value
    payload[:, :local] = value.astype(BF16)
    payload[:, local:] = lanes_of([jnp.sum(value * value, axis=1, keepdims=True)], rows)
    lane = lax.broadcasted_iota(jnp.int32, scalars.shape, 1)
    scalars[...] = jnp.where(lane == 0, alpha, beta)


def data_last_body(n_col, n_row, data_prev, *refs):
    pieces, (square, scalars) = refs[:n_col], refs[n_col:]
    rows, local = data_prev.shape
    alpha, beta = scalars_of(pieces, local, n_col, n_row)
    value = total_of(pieces, slice(None), slice(0, local)) / alpha - (alpha / beta) * data_prev[...]
    square[...] = jnp.broadcast_to(jnp.sum(value * value, axis=1, keepdims=True), square.shape)
    lane = lax.broadcasted_iota(jnp.int32, scalars.shape, 1)
    scalars[...] = jnp.where(lane == 0, alpha, beta)


def add_body(*refs):
    refs[-1][...] = sum(ref[...] for ref in refs[:-1])


def pick_body(n_col, place, where, *refs):
    firsts, seconds, (out, scr) = refs[:n_col], refs[n_col : 2 * n_col], refs[2 * n_col :]
    rows = firsts[0].shape[0]
    width = out.shape[1]
    tile_cols = where.shape[0]
    tile = width // tile_cols
    for j in range(n_col):
        scr[j, :rows] = firsts[j][:, :width]
        scr[j, rows:] = seconds[j][:, :width]
    for p in range(tile_cols):
        held = where[p]
        source = jnp.bitwise_xor(held // tile_cols, place[0])
        at = pl.multiple_of((held % tile_cols) * tile, tile)
        out[:, p * tile : (p + 1) * tile] = scr[source, :, pl.ds(at, tile)]


def finish_body(n_row, place, *refs):
    squares, pieces = refs[:n_row], refs[n_row : 2 * n_row]
    scal_first, scal_next, solution, residual = refs[2 * n_row :]
    rows = squares[0].shape[0]
    total = squares[0][...]
    for k in range(1, n_row):
        other = squares[k][...].reshape(n_row, rows // n_row, squares[k].shape[1])
        moved = jnp.stack([other[g ^ k] for g in range(n_row)], axis=0)
        total = total + moved.reshape(total.shape)
    half = rows // (2 * n_row)
    beta_last = jnp.sqrt(both_parts(total[:, 0:1], half))
    alpha_0, beta_0 = scal_first[:, 0:1], scal_first[:, 1:2]
    alpha_1, beta_1 = scal_next[:, 0:1], scal_next[:, 1:2]
    rho = jnp.sqrt(alpha_0 * alpha_0 + beta_1 * beta_1)
    cosine = alpha_0 / rho
    sine = beta_1 / rho
    theta = sine * alpha_1
    rhobar = -cosine * alpha_1
    phi = cosine * beta_0
    phibar = sine * beta_0
    first = phi / rho
    slope = theta / rho
    rho = jnp.sqrt(rhobar * rhobar + beta_last * beta_last)
    second = (rhobar / rho) * phibar / rho
    phibar = (beta_last / rho) * phibar
    weight_0 = (first - second * slope) / alpha_0
    weight_1 = second / alpha_1
    for k in range(n_row):
        held = jnp.bitwise_xor(place[1], k)
        at = pl.multiple_of(held * half, half)
        lo, hi = 2 * half * k, 2 * half * (k + 1)
        v_0 = pieces[k][: 2 * half, :].astype(F32)
        v_1 = pieces[k][2 * half :, :].astype(F32)
        mixed = weight_0[lo:hi] * v_0 + weight_1[lo:hi] * v_1
        for part in range(2):
            solution[part, pl.ds(at, half), :] = mixed[part * half : (part + 1) * half]
        residual[pl.ds(at, half), :] = jnp.broadcast_to(phibar[lo : lo + half], (half, residual.shape[1]))


def swap(value, axis, size, mask):
    return lax.ppermute(value, axis, [(j, j ^ mask) for j in range(size)])


def scatter(pieces, axis, size):
    return [pieces[0]] + [swap(pieces[k], axis, size, k) for k in range(1, size)]


def gather_row(value, size):
    return [value] + [swap(value, "row", size, k) for k in range(1, size)]


def gather_col(value, size):
    even = {0: value}
    for k in range(2, size, 2):
        even[k] = swap(value, "col", size, k)
    pieces = []
    for k in range(0, size, 2):
        pieces += [even[k], swap(even[k], "col", size, 1)]
    return pieces


def on_device(rhs, u_factor, v_factor, ranks, assign):
    n_col, n_row = lax.axis_size("col"), lax.axis_size("row")
    tile_rows, tile_cols, _, tile_size, _ = u_factor.shape
    sources, local = rhs.shape[1], rhs.shape[3]
    rows = 2 * sources
    share = rows // n_row
    width = tile_cols * tile_size
    place = jnp.stack([lax.axis_index("col"), lax.axis_index("row")]).astype(jnp.int32)
    shape = jax.ShapeDtypeStruct
    data_shape, model_shape = shape((rows, local + EXT), BF16), shape((share, width + EXT), BF16)
    scalar_shape = shape((rows, EXT), F32)

    adjoint = functools.partial(
        product,
        functools.partial(adjoint_body, n_col, n_row),
        place,
        ranks,
        u_factor,
        v_factor,
        out_shapes=[model_shape] * n_row,
        scratch=[pltpu.VMEM((tile_rows, rows, tile_size), BF16), pltpu.VMEM((rows, width), F32)],
    )
    forward = functools.partial(
        product,
        functools.partial(forward_body, n_col, n_row),
        place,
        ranks,
        u_factor,
        v_factor,
        out_shapes=[data_shape] * n_col,
        scratch=[pltpu.VMEM((rows, width + EXT), BF16), pltpu.VMEM((tile_rows, rows, tile_size), BF16)],
    )

    data_0, payload = small(
        functools.partial(begin_body, n_row),
        [shape((rows, local), F32), data_shape],
        place,
        rhs.reshape(2, sources, local),
    )
    partial_model = adjoint(gather_col(payload, n_col))
    v_hat_0, model_0 = small(
        functools.partial(model_first_body, n_row),
        [shape((share, width), F32), model_shape],
        *scatter(partial_model, "row", n_row),
    )
    partial_data = forward(gather_row(model_0, n_row))
    data_1, payload, scal_first = small(
        functools.partial(data_next_body, n_col, n_row),
        [shape((rows, local), F32), data_shape, scalar_shape],
        data_0,
        *scatter(partial_data, "col", n_col),
    )
    partial_model = adjoint(gather_col(payload, n_col))
    (model_1,) = small(
        functools.partial(model_next_body, n_row),
        [model_shape],
        v_hat_0,
        scal_first,
        *scatter(partial_model, "row", n_row),
    )
    partial_data = forward(gather_row(model_1, n_row))

    natural = lax.axis_index("col") * tile_cols + jnp.arange(tile_cols, dtype=jnp.int32)
    positions = jnp.arange(assign.shape[0], dtype=jnp.int32)
    where_held = jnp.sum(
        positions[None, :] * (assign[None, :] == natural[:, None]).astype(jnp.int32), axis=1
    )
    held = gather_col(model_0, n_col) + gather_col(model_1, n_col)
    picked = pl.pallas_call(
        functools.partial(pick_body, n_col),
        in_specs=[SMEM, SMEM] + [VMEM] * (2 * n_col),
        out_specs=VMEM,
        out_shape=shape((2 * share, width), BF16),
        scratch_shapes=[pltpu.VMEM((n_col, 2 * share, width), BF16)],
        compiler_params=PARAMS,
    )(place, where_held, *held)
    blocks = gather_row(picked, n_row)

    square, scal_next = small(
        functools.partial(data_last_body, n_col, n_row),
        [scalar_shape, scalar_shape],
        data_1,
        *scatter(partial_data, "col", n_col),
    )
    (square,) = small(add_body, [scalar_shape], square, swap(square, "col", n_col, 1))
    (square,) = small(
        add_body, [scalar_shape], square, *[swap(square, "col", n_col, k) for k in range(2, n_col, 2)]
    )
    solution, residual = small(
        functools.partial(finish_body, n_row),
        [shape((2, sources, width), F32), shape((sources, EXT), F32)],
        place,
        *gather_row(square, n_row),
        *blocks,
        scal_first,
        scal_next,
    )
    return (solution, residual[:, 0])


def solution(mesh):
    in_specs = (
        P(None, None, "row", "col"),
        P("row", "col", None, None, None),
        P("row", "col", None, None, None),
        P("row", "col"),
        P(),
    )
    out_specs = (P(None, None, "col"), P())
    return jax.shard_map(
        on_device, mesh=mesh, in_specs=in_specs, out_specs=out_specs, check_vma=False
    )
```

time: 340 us -> 187 us (0.55)
  blocking collectives: 190 us -> 0 us
  Pallas kernels: 0 us -> 73.3 us
  starting transfers between devices: 0.16 us -> 57.6 us
  matrix products: 40 us -> 0 us
  waiting for transfers between devices: 70.1 us -> 51.5 us
  other arithmetic: 16.8 us -> 0.26 us
  between operations: 14.3 us -> 0.88 us
  local copies, waits for them, and re-layouts: 7.14 us -> 2.31 us
    psum x5 -> x0, blocking collectives: 144 us -> none  [the longest x3 119 us: adjoint_step(): beta_now = jnp.sqrt(lax.psum(sum_squares(data_hat), ('col', 'row')))]
    pallas_call x0 -> x13, Pallas kernels: none -> 73.3 us  [the longest x4 69.3 us: product(): pl.pallas_call(body, grid_spec=pltpu.PrefetchScalarGridSpec(num_scalar_pr...]
    reduce_scatter x2 -> x0, waiting for transfers between devices: 70 us -> none  [on_device(): lax.psum_scatter(partial_data, 'col', scatter_dimension=2, tiled=True)]
    ppermute x0 -> x64, starting transfers between devices: none -> 57.6 us  [swap(): return lax.ppermute(value, axis, [(j, j ^ mask) for j in range(size)])]
    ppermute x0 -> x64, waiting for transfers between devices: none -> 51.5 us  [swap(): return lax.ppermute(value, axis, [(j, j ^ mask) for j in range(size)])]
    all_gather x4 -> x0, blocking collectives: 46.5 us -> none  [the longest x2 21.3 us: adjoint_step(): lax.all_gather(data_hat.astype(jnp.bfloat16), 'col', axis=2, tiled=True)]
    dot_general x8 -> x0, matrix products: 40 us -> none  [the longest x2 11.3 us: adjoint_terms(): jnp.einsum('ipcnk,dsin->ipcdsk', u_factor, data_b, preferred_element_type...]
    reduce_sum x5 -> x0, other arithmetic: 4.89 us -> none  [sum_squares(): return jnp.sum(value * value, axis=(0, 2))]
  transfers between devices with their start and end apart: 4 -> 64, of which waited for: 2 -> 31; matrix products, arithmetic and copies ran while one was open for 0% -> 1% of each run, Pallas kernels for 0% -> 10%
where the time goes in v1:
time: 187 us; the launch traced here: 186 us
  Pallas kernels  73.3 us (39%)
  starting transfers between devices  57.6 us (31%)
  waiting for transfers between devices  51.5 us (28%)
  local copies, waits for them, and re-layouts  2.31 us (1%)
    pallas_call x4, Pallas kernels, product(): pl.pallas_call(body, grid_spec=pltpu.PrefetchScalarGridSpec(num_scalar_pr...  69.3 us
    ppermute x64, starting transfers between devices, swap(): return lax.ppermute(value, axis, [(j, j ^ mask) for j in range(size)])  57.6 us
    ppermute x64, waiting for transfers between devices, swap(): return lax.ppermute(value, axis, [(j, j ^ mask) for j in range(size)])  51.5 us
  transfers between devices with their start and end apart: 64, of which 31 were waited for; matrix products, arithmetic and copies ran while one was open for 1% of the time, Pallas kernels for 10%

profile of v1, /device:TPU:0, one launch (start us, length us, event | category | flops | bytes accessed | tf_op | source)
XLA Modules:
  0.0 185.8 jit_solution(12072306298209277779)
XLA Ops:
  2.3 3.0 %collective-permute-start.1 = (bf16[64,640]{1,0:T(8,128)(2,1)S(1)}, bf16[64,640]{1,0:T(8,128)(2,1)S(1)}, u32[]{:S(2)}, u32[]{:S(2)}) collective-permute-start(bf16[64,640]{1,0:T(8,128)(2,1)S(1)} %get-tuple-element.38.refs_0_), channel_id=1, source_target_pairs={{0,8},{4,12},{8,0},{12,4},{16,24},{20,28},{24,16},{28,20},{1,9},{5... | collective-permute-start | bytes 245768 | tf_op jit(solution)/shard_map/ppermute | solution.py:301
  8.0 2.6 %collective-permute-done.3.refs_4_ = bf16[64,640]{1,0:T(8,128)(2,1)S(1)} collective-permute-done((bf16[64,640]{1,0:T(8,128)(2,1)S(1)}, bf16[64,640]{1,0:T(8,128)(2,1)S(1)}, u32[]{:S(2)}, u32[]{:S(2)}) %collective-permute-start.3) | collective-permute-done | bytes 81952 | tf_op jit(solution)/shard_map/ppermute | solution.py:301
  13.4 17.3 %shard_map.69 = (bf16[16,1408]{1,0:T(8,128)(2,1)S(1)}, bf16[16,1408]{1,0:T(8,128)(2,1)S(1)}, bf16[16,1408]{1,0:T(8,128)(2,1)S(1)}, bf16[16,1408]{1,0:T(8,128)(2,1)S(1)}) custom-call(s32[2]{0:T(128)S(1)} %pad_add_fusion.place, s32[16,5]{1,0:T(8,128)S(1)} %copy.16.ranks, bf16[16,5,2,256,128]{4,3,2,1,0:T(8,128)(2,1)} %u_ref.7, ...), custom_call_target="tpu_custom_call" | custom-call | tf_op jit(solution)/shard_map/pallas_call | solution.py:148
  32.4 2.6 %collective-permute-start.8 = (bf16[16,1408]{1,0:T(8,128)(2,1)S(1)}, bf16[16,1408]{1,0:T(8,128)(2,1)S(1)}, u32[]{:S(2)}, u32[]{:S(2)}) collective-permute-start(bf16[16,1408]{1,0:T(8,128)(2,1)S(1)} %get-tuple-element.41), channel_id=1, source_target_pairs={{0,2},{1,3},{2,0},{3,1},{4,6},{5,7},{6,4},{7,5},{8,10},{9,11},{10,... | collective-permute-start | bytes 135176 | tf_op jit(solution)/shard_map/ppermute | solution.py:301
  35.2 2.9 %collective-permute-done.8.refs_2_ = bf16[16,1408]{1,0:T(8,128)(2,1)S(1)} collective-permute-done((bf16[16,1408]{1,0:T(8,128)(2,1)S(1)}, bf16[16,1408]{1,0:T(8,128)(2,1)S(1)}, u32[]{:S(2)}, u32[]{:S(2)}) %collective-permute-start.8) | collective-permute-done | bytes 45088 | tf_op jit(solution)/shard_map/ppermute | solution.py:301
  38.1 2.7 %collective-permute-done.9.refs_3_ = bf16[16,1408]{1,0:T(8,128)(2,1)S(1)} collective-permute-done((bf16[16,1408]{1,0:T(8,128)(2,1)S(1)}, bf16[16,1408]{1,0:T(8,128)(2,1)S(1)}, u32[]{:S(2)}, u32[]{:S(2)}) %collective-permute-start.9) | collective-permute-done | bytes 45088 | tf_op jit(solution)/shard_map/ppermute | solution.py:301
  42.5 3.0 %collective-permute-start.12 = (bf16[16,1408]{1,0:T(8,128)(2,1)S(1)}, bf16[16,1408]{1,0:T(8,128)(2,1)S(1)}, u32[]{:S(2)}, u32[]{:S(2)}) collective-permute-start(bf16[16,1408]{1,0:T(8,128)(2,1)S(1)} %get-tuple-element.43.refs_0_), channel_id=1, source_target_pairs={{0,3},{1,2},{2,1},{3,0},{4,7},{5,6},{6,5},{7,4},{8,11},{9,10},{10,... | collective-permute-start | bytes 135176 | tf_op jit(solution)/shard_map/ppermute | solution.py:301
  46.1 2.2 %collective-permute-done.12.refs_3_ = bf16[16,1408]{1,0:T(8,128)(2,1)S(1)} collective-permute-done((bf16[16,1408]{1,0:T(8,128)(2,1)S(1)}, bf16[16,1408]{1,0:T(8,128)(2,1)S(1)}, u32[]{:S(2)}, u32[]{:S(2)}) %collective-permute-start.12) | collective-permute-done | bytes 45088 | tf_op jit(solution)/shard_map/ppermute | solution.py:301
  48.3 17.4 %shard_map.71 = (bf16[64,640]{1,0:T(8,128)(2,1)S(1)}, bf16[64,640]{1,0:T(8,128)(2,1)S(1)}, bf16[64,640]{1,0:T(8,128)(2,1)S(1)}, bf16[64,640]{1,0:T(8,128)(2,1)S(...) custom-call(s32[2]{0:T(128)S(1)} %pad_add_fusion.place, ...), custom_call_target="tpu_custom_call" | custom-call | tf_op jit(solution)/shard_map/pallas_call | solution.py:148
  72.9 4.0 %collective-permute-done.17.refs_5_ = bf16[64,640]{1,0:T(8,128)(2,1)S(1)} collective-permute-done((bf16[64,640]{1,0:T(8,128)(2,1)S(1)}, bf16[64,640]{1,0:T(8,128)(2,1)S(1)}, u32[]{:S(2)}, u32[]{:S(2)}) %collective-permute-start.17) | collective-permute-done | bytes 81952 | tf_op jit(solution)/shard_map/ppermute | solution.py:301
  78.9 1.9 %collective-permute-start.25 = (bf16[64,640]{1,0:T(8,128)(2,1)S(1)}, bf16[64,640]{1,0:T(8,128)(2,1)S(1)}, u32[]{:S(2)}, u32[]{:S(2)}) collective-permute-start(bf16[64,640]{1,0:T(8,128)(2,1)S(1)} %get-tuple-element.55.refs_0_), channel_id=1, source_target_pairs={{0,24},{4,28},{8,16},{12,20},{16,8},{20,12},{24,0},{28,4},{1,25},{... | collective-permute-start | bytes 245768 | tf_op jit(solution)/shard_map/ppermute | solution.py:301
  85.6 17.3 %shard_map.73 = (bf16[16,1408]{1,0:T(8,128)(2,1)S(1)}, bf16[16,1408]{1,0:T(8,128)(2,1)S(1)}, bf16[16,1408]{1,0:T(8,128)(2,1)S(1)}, bf16[16,1408]{1,0:T(8,128)(2,1)S(1)}) custom-call(s32[2]{0:T(128)S(1)} %pad_add_fusion.place, s32[16,5]{1,0:T(8,128)S(1)} %copy.16.ranks, bf16[16,5,2,256,128]{4,3,2,1,0:T(8,128)(2,1)} %u_ref.7, ...), custom_call_target="tpu_custom_call" | custom-call | tf_op jit(solution)/shard_map/pallas_call | solution.py:148
  102.9 3.6 %collective-permute-start.28 = (bf16[16,1408]{1,0:T(8,128)(2,1)S(1)}, bf16[16,1408]{1,0:T(8,128)(2,1)S(1)}, u32[]{:S(2)}, u32[]{:S(2)}) collective-permute-start(bf16[16,1408]{1,0:T(8,128)(2,1)S(1)} %get-tuple-element.58), channel_id=1, source_target_pairs={{0,2},{1,3},{2,0},{3,1},{4,6},{5,7},{6,4},{7,5},{8,10},{9,11},{10,... | collective-permute-start | bytes 135176 | tf_op jit(solution)/shard_map/ppermute | solution.py:301
  107.3 2.3 %collective-permute-done.28.refs_2_ = bf16[16,1408]{1,0:T(8,128)(2,1)S(1)} collective-permute-done((bf16[16,1408]{1,0:T(8,128)(2,1)S(1)}, bf16[16,1408]{1,0:T(8,128)(2,1)S(1)}, u32[]{:S(2)}, u32[]{:S(2)}) %collective-permute-start.28) | collective-permute-done | bytes 45088 | tf_op jit(solution)/shard_map/ppermute | solution.py:301
  109.5 2.8 %collective-permute-done.29.refs_3_ = bf16[16,1408]{1,0:T(8,128)(2,1)S(1)} collective-permute-done((bf16[16,1408]{1,0:T(8,128)(2,1)S(1)}, bf16[16,1408]{1,0:T(8,128)(2,1)S(1)}, u32[]{:S(2)}, u32[]{:S(2)}) %collective-permute-start.29) | collective-permute-done | bytes 45088 | tf_op jit(solution)/shard_map/ppermute | solution.py:301
  114.1 2.9 %collective-permute-start.32 = (bf16[16,1408]{1,0:T(8,128)(2,1)S(1)}, bf16[16,1408]{1,0:T(8,128)(2,1)S(1)}, u32[]{:S(2)}, u32[]{:S(2)}) collective-permute-start(bf16[16,1408]{1,0:T(8,128)(2,1)S(1)} %shard_map.74.refs_0_.refs_8_), channel_id=1, source_target_pairs={{0,3},{1,2},{2,1},{3,0},{4,7},{5,6},{6,5},{7,4},{8,11},{9,10},{10,... | collective-permute-start | bytes 135176 | tf_op jit(solution)/shard_map/ppermute | solution.py:301
  120.0 17.4 %shard_map.75 = (bf16[64,640]{1,0:T(8,128)(2,1)S(1)}, bf16[64,640]{1,0:T(8,128)(2,1)S(1)}, bf16[64,640]{1,0:T(8,128)(2,1)S(1)}, bf16[64,640]{1,0:T(8,128)(2,1)S(...) custom-call(s32[2]{0:T(128)S(1)} %pad_add_fusion.place, ...), custom_call_target="tpu_custom_call" | custom-call | tf_op jit(solution)/shard_map/pallas_call | solution.py:148
  142.8 2.0 %collective-permute-done.52.refs_6_ = bf16[16,1408]{1,0:T(8,128)(2,1)S(1)} collective-permute-done((bf16[16,1408]{1,0:T(8,128)(2,1)S(1)}, bf16[16,1408]{1,0:T(8,128)(2,1)S(1)}, u32[]{:S(2)}, u32[]{:S(2)}) %collective-permute-start.52) | collective-permute-done | bytes 45088 | tf_op jit(solution)/shard_map/ppermute | solution.py:301
  147.0 2.2 %collective-permute-start.39 = (bf16[64,640]{1,0:T(8,128)(2,1)S(1)}, bf16[64,640]{1,0:T(8,128)(2,1)S(1)}, u32[]{:S(2)}, u32[]{:S(2)}) collective-permute-start(bf16[64,640]{1,0:T(8,128)(2,1)S(1)} %get-tuple-element.67), channel_id=1, source_target_pairs={{0,28},{4,24},{8,20},{12,16},{16,12},{20,8},{24,4},{28,0},{1,29},{... | collective-permute-start | bytes 245768 | tf_op jit(solution)/shard_map/ppermute | solution.py:301
  149.8 4.2 %collective-permute-done.37.refs_5_ = bf16[64,640]{1,0:T(8,128)(2,1)S(1)} collective-permute-done((bf16[64,640]{1,0:T(8,128)(2,1)S(1)}, bf16[64,640]{1,0:T(8,128)(2,1)S(1)}, u32[]{:S(2)}, u32[]{:S(2)}) %collective-permute-start.37) | collective-permute-done | bytes 81952 | tf_op jit(solution)/shard_map/ppermute | solution.py:301
  158.8 1.9 %collective-permute-done.59.refs_14_ = bf16[16,1408]{1,0:T(8,128)(2,1)S(1)} collective-permute-done((bf16[16,1408]{1,0:T(8,128)(2,1)S(1)}, bf16[16,1408]{1,0:T(8,128)(2,1)S(1)}, u32[]{:S(2)}, u32[]{:S(2)}) %collective-permute-start.59) | collective-permute-done | bytes 45088 | tf_op jit(solution)/shard_map/ppermute | solution.py:301
  164.1 3.5 %collective-permute-start.62 = (bf16[32,1280]{1,0:T(8,128)(2,1)S(1)}, bf16[32,1280]{1,0:T(8,128)(2,1)S(1)}, u32[]{:S(2)}, u32[]{:S(2)}) collective-permute-start(bf16[32,1280]{1,0:T(8,128)(2,1)S(1)} %shard_map.79.refs_4_), channel_id=1, source_target_pairs={{0,2},{1,3},{2,0},{3,1},{4,6},{5,7},{6,4},{7,5},{8,10},{9,11},{10,... | collective-permute-start | bytes 245768 | tf_op jit(solution)/shard_map/ppermute | solution.py:301
  174.3 3.5 %collective-permute-start.45 = (f32[64,128]{1,0:T(8,128)S(1)}, f32[64,128]{1,0:T(8,128)S(1)}, u32[]{:S(2)}, u32[]{:S(2)}) collective-permute-start(f32[64,128]{1,0:T(8,128)S(1)} %shard_map.78.refs_0_), channel_id=1, source_target_pairs={{0,2},{1,3},{2,0},{3,1},{4,6},{5,7},{6,4},{7,5},{8,10},{9,11},{10,... | collective-permute-start | bytes 98312 | tf_op jit(solution)/shard_map/ppermute | solution.py:301
  180.1 3.5 %collective-permute-done.46.refs_3_ = f32[64,128]{1,0:T(8,128)S(1)} collective-permute-done((f32[64,128]{1,0:T(8,128)S(1)}, f32[64,128]{1,0:T(8,128)S(1)}, u32[]{:S(2)}, u32[]{:S(2)}) %collective-permute-start.46) | collective-permute-done | bytes 32800 | tf_op jit(solution)/shard_map/ppermute | solution.py:301
  (125 shorter events, 58.2 us)
Async XLA Ops:
  6.9 6.1 %collective-permute-start = (bf16[64,640]{1,0:T(8,128)(2,1)S(1)}, bf16[64,640]{1,0:T(8,128)(2,1)S(1)}, u32[]{:S(2)}, u32[]{:S(2)}) collective-permute-start(bf16[64,640]{1,0:T(8,128)(2,1)S(1)} %get-tuple-element.38.refs_0_), channel_id=1, source_target_pairs={{0,4},{4,0},{8,12},{12,8},{16,20},{20,16},{24,28},{28,24},{1,5},{5... | collective-permute-start | bytes 245768 | tf_op jit(solution)/shard_map/ppermute | solution.py:301
  34.9 5.8 %collective-permute-start.9 = (bf16[16,1408]{1,0:T(8,128)(2,1)S(1)}, bf16[16,1408]{1,0:T(8,128)(2,1)S(1)}, u32[]{:S(2)}, u32[]{:S(2)}) collective-permute-start(bf16[16,1408]{1,0:T(8,128)(2,1)S(1)} %get-tuple-element.42), channel_id=1, source_target_pairs={{0,3},{1,2},{2,1},{3,0},{4,7},{5,6},{6,5},{7,4},{8,11},{9,10},{10,... | collective-permute-start | bytes 135176 | tf_op jit(solution)/shard_map/ppermute | solution.py:301
  42.5 5.8 %collective-permute-start.12 = (bf16[16,1408]{1,0:T(8,128)(2,1)S(1)}, bf16[16,1408]{1,0:T(8,128)(2,1)S(1)}, u32[]{:S(2)}, u32[]{:S(2)}) collective-permute-start(bf16[16,1408]{1,0:T(8,128)(2,1)S(1)} %get-tuple-element.43.refs_0_), channel_id=1, source_target_pairs={{0,3},{1,2},{2,1},{3,0},{4,7},{5,6},{6,5},{7,4},{8,11},{9,10},{10,... | collective-permute-start | bytes 135176 | tf_op jit(solution)/shard_map/ppermute | solution.py:301
  68.2 8.8 %collective-permute-start.17 = (bf16[64,640]{1,0:T(8,128)(2,1)S(1)}, bf16[64,640]{1,0:T(8,128)(2,1)S(1)}, u32[]{:S(2)}, u32[]{:S(2)}) collective-permute-start(bf16[64,640]{1,0:T(8,128)(2,1)S(1)} %get-tuple-element.49), channel_id=1, source_target_pairs={{0,20},{4,16},{8,28},{12,24},{16,4},{20,0},{24,12},{28,8},{1,21},{... | collective-permute-start | bytes 245768 | tf_op jit(solution)/shard_map/ppermute | solution.py:301
  69.3 7.6 %collective-permute-start.18 = (bf16[64,640]{1,0:T(8,128)(2,1)S(1)}, bf16[64,640]{1,0:T(8,128)(2,1)S(1)}, u32[]{:S(2)}, u32[]{:S(2)}) collective-permute-start(bf16[64,640]{1,0:T(8,128)(2,1)S(1)} %get-tuple-element.50), channel_id=1, source_target_pairs={{0,24},{4,28},{8,16},{12,20},{16,8},{20,12},{24,0},{28,4},{1,25},{... | collective-permute-start | bytes 245768 | tf_op jit(solution)/shard_map/ppermute | solution.py:301
  71.2 5.8 %collective-permute-start.19 = (bf16[64,640]{1,0:T(8,128)(2,1)S(1)}, bf16[64,640]{1,0:T(8,128)(2,1)S(1)}, u32[]{:S(2)}, u32[]{:S(2)}) collective-permute-start(bf16[64,640]{1,0:T(8,128)(2,1)S(1)} %get-tuple-element.51), channel_id=1, source_target_pairs={{0,28},{4,24},{8,20},{12,16},{16,12},{20,8},{24,4},{28,0},{1,29},{... | collective-permute-start | bytes 245768 | tf_op jit(solution)/shard_map/ppermute | solution.py:301
  102.9 6.6 %collective-permute-start.28 = (bf16[16,1408]{1,0:T(8,128)(2,1)S(1)}, bf16[16,1408]{1,0:T(8,128)(2,1)S(1)}, u32[]{:S(2)}, u32[]{:S(2)}) collective-permute-start(bf16[16,1408]{1,0:T(8,128)(2,1)S(1)} %get-tuple-element.58), channel_id=1, source_target_pairs={{0,2},{1,3},{2,0},{3,1},{4,6},{5,7},{6,4},{7,5},{8,10},{9,11},{10,... | collective-permute-start | bytes 135176 | tf_op jit(solution)/shard_map/ppermute | solution.py:301
  106.5 5.8 %collective-permute-start.29 = (bf16[16,1408]{1,0:T(8,128)(2,1)S(1)}, bf16[16,1408]{1,0:T(8,128)(2,1)S(1)}, u32[]{:S(2)}, u32[]{:S(2)}) collective-permute-start(bf16[16,1408]{1,0:T(8,128)(2,1)S(1)} %get-tuple-element.59), channel_id=1, source_target_pairs={{0,3},{1,2},{2,1},{3,0},{4,7},{5,6},{6,5},{7,4},{8,11},{9,10},{10,... | collective-permute-start | bytes 135176 | tf_op jit(solution)/shard_map/ppermute | solution.py:301
  112.6 5.8 %collective-permute-start.30 = (bf16[16,1408]{1,0:T(8,128)(2,1)S(1)}, bf16[16,1408]{1,0:T(8,128)(2,1)S(1)}, u32[]{:S(2)}, u32[]{:S(2)}) collective-permute-start(bf16[16,1408]{1,0:T(8,128)(2,1)S(1)} %shard_map.74.refs_0_.refs_8_), channel_id=1, source_target_pairs={{0,1},{1,0},{2,3},{3,2},{4,5},{5,4},{6,7},{7,6},{8,9},{9,8},{10,11... | collective-permute-start | bytes 135176 | tf_op jit(solution)/shard_map/ppermute | solution.py:301
  114.1 5.8 %collective-permute-start.32 = (bf16[16,1408]{1,0:T(8,128)(2,1)S(1)}, bf16[16,1408]{1,0:T(8,128)(2,1)S(1)}, u32[]{:S(2)}, u32[]{:S(2)}) collective-permute-start(bf16[16,1408]{1,0:T(8,128)(2,1)S(1)} %shard_map.74.refs_0_.refs_8_), channel_id=1, source_target_pairs={{0,3},{1,2},{2,1},{3,0},{4,7},{5,6},{6,5},{7,4},{8,11},{9,10},{10,... | collective-permute-start | bytes 135176 | tf_op jit(solution)/shard_map/ppermute | solution.py:301
  117.1 22.8 %collective-permute-start.47 = (bf16[16,1408]{1,0:T(8,128)(2,1)S(1)}, bf16[16,1408]{1,0:T(8,128)(2,1)S(1)}, u32[]{:S(2)}, u32[]{:S(2)}) collective-permute-start(bf16[16,1408]{1,0:T(8,128)(2,1)S(1)} %get-tuple-element.43.refs_0_), channel_id=1, source_target_pairs={{0,4},{4,0},{8,12},{12,8},{16,20},{20,16},{24,28},{28,24},{1,5},{5... | collective-permute-start | bytes 135176 | tf_op jit(solution)/shard_map/ppermute | solution.py:301
  117.1 23.9 %collective-permute-start.48 = (bf16[16,1408]{1,0:T(8,128)(2,1)S(1)}, bf16[16,1408]{1,0:T(8,128)(2,1)S(1)}, u32[]{:S(2)}, u32[]{:S(2)}) collective-permute-start(bf16[16,1408]{1,0:T(8,128)(2,1)S(1)} %get-tuple-element.43.refs_0_), channel_id=1, source_target_pairs={{0,8},{4,12},{8,0},{12,4},{16,24},{20,28},{24,16},{28,20},{1,9},{5... | collective-permute-start | bytes 135176 | tf_op jit(solution)/shard_map/ppermute | solution.py:301
  137.4 8.4 %collective-permute-start.33 = (bf16[64,640]{1,0:T(8,128)(2,1)S(1)}, bf16[64,640]{1,0:T(8,128)(2,1)S(1)}, u32[]{:S(2)}, u32[]{:S(2)}) collective-permute-start(bf16[64,640]{1,0:T(8,128)(2,1)S(1)} %get-tuple-element.61), channel_id=1, source_target_pairs={{0,4},{4,0},{8,12},{12,8},{16,20},{20,16},{24,28},{28,24},{1,5},{5... | collective-permute-start | bytes 245768 | tf_op jit(solution)/shard_map/ppermute | solution.py:301
  137.4 9.6 %collective-permute-start.34 = (bf16[64,640]{1,0:T(8,128)(2,1)S(1)}, bf16[64,640]{1,0:T(8,128)(2,1)S(1)}, u32[]{:S(2)}, u32[]{:S(2)}) collective-permute-start(bf16[64,640]{1,0:T(8,128)(2,1)S(1)} %get-tuple-element.62), channel_id=1, source_target_pairs={{0,8},{4,12},{8,0},{12,4},{16,24},{20,28},{24,16},{28,20},{1,9},{5... | collective-permute-start | bytes 245768 | tf_op jit(solution)/shard_map/ppermute | solution.py:301
  142.8 6.4 %collective-permute-start.35 = (bf16[64,640]{1,0:T(8,128)(2,1)S(1)}, bf16[64,640]{1,0:T(8,128)(2,1)S(1)}, u32[]{:S(2)}, u32[]{:S(2)}) collective-permute-start(bf16[64,640]{1,0:T(8,128)(2,1)S(1)} %get-tuple-element.63), channel_id=1, source_target_pairs={{0,12},{4,8},{8,4},{12,0},{16,28},{20,24},{24,20},{28,16},{1,13},{... | collective-permute-start | bytes 245768 | tf_op jit(solution)/shard_map/ppermute | solution.py:301
  145.8 8.3 %collective-permute-start.37 = (bf16[64,640]{1,0:T(8,128)(2,1)S(1)}, bf16[64,640]{1,0:T(8,128)(2,1)S(1)}, u32[]{:S(2)}, u32[]{:S(2)}) collective-permute-start(bf16[64,640]{1,0:T(8,128)(2,1)S(1)} %get-tuple-element.65), channel_id=1, source_target_pairs={{0,20},{4,16},{8,28},{12,24},{16,4},{20,0},{24,12},{28,8},{1,21},{... | collective-permute-start | bytes 245768 | tf_op jit(solution)/shard_map/ppermute | solution.py:301
  145.8 9.0 %collective-permute-start.38 = (bf16[64,640]{1,0:T(8,128)(2,1)S(1)}, bf16[64,640]{1,0:T(8,128)(2,1)S(1)}, u32[]{:S(2)}, u32[]{:S(2)}) collective-permute-start(bf16[64,640]{1,0:T(8,128)(2,1)S(1)} %get-tuple-element.66), channel_id=1, source_target_pairs={{0,24},{4,28},{8,16},{12,20},{16,8},{20,12},{24,0},{28,4},{1,25},{... | collective-permute-start | bytes 245768 | tf_op jit(solution)/shard_map/ppermute | solution.py:301
  147.0 8.7 %collective-permute-start.39 = (bf16[64,640]{1,0:T(8,128)(2,1)S(1)}, bf16[64,640]{1,0:T(8,128)(2,1)S(1)}, u32[]{:S(2)}, u32[]{:S(2)}) collective-permute-start(bf16[64,640]{1,0:T(8,128)(2,1)S(1)} %get-tuple-element.67), channel_id=1, source_target_pairs={{0,28},{4,24},{8,20},{12,16},{16,12},{20,8},{24,4},{28,0},{1,29},{... | collective-permute-start | bytes 245768 | tf_op jit(solution)/shard_map/ppermute | solution.py:301
  149.2 8.6 %collective-permute-start.51 = (bf16[16,1408]{1,0:T(8,128)(2,1)S(1)}, bf16[16,1408]{1,0:T(8,128)(2,1)S(1)}, u32[]{:S(2)}, u32[]{:S(2)}) collective-permute-start(bf16[16,1408]{1,0:T(8,128)(2,1)S(1)} %collective-permute-done.50.refs_4_), channel_id=1, source_target_pairs={{0,4},{4,0},{8,12},{12,8},{16,20},{20,16},{24,28},{28,24},{1,5},{5... | collective-permute-start | bytes 135176 | tf_op jit(solution)/shard_map/ppermute | solution.py:301
  149.8 10.9 %collective-permute-start.53 = (bf16[16,1408]{1,0:T(8,128)(2,1)S(1)}, bf16[16,1408]{1,0:T(8,128)(2,1)S(1)}, u32[]{:S(2)}, u32[]{:S(2)}) collective-permute-start(bf16[16,1408]{1,0:T(8,128)(2,1)S(1)} %collective-permute-done.52.refs_6_), channel_id=1, source_target_pairs={{0,4},{4,0},{8,12},{12,8},{16,20},{20,16},{24,28},{28,24},{1,5},{5... | collective-permute-start | bytes 135176 | tf_op jit(solution)/shard_map/ppermute | solution.py:301
  162.5 15.3 %collective-permute-start.61 = (bf16[32,1280]{1,0:T(8,128)(2,1)S(1)}, bf16[32,1280]{1,0:T(8,128)(2,1)S(1)}, u32[]{:S(2)}, u32[]{:S(2)}) collective-permute-start(bf16[32,1280]{1,0:T(8,128)(2,1)S(1)} %shard_map.79.refs_4_), channel_id=1, source_target_pairs={{0,1},{1,0},{2,3},{3,2},{4,5},{5,4},{6,7},{7,6},{8,9},{9,8},{10,11... | collective-permute-start | bytes 245768 | tf_op jit(solution)/shard_map/ppermute | solution.py:301
  162.7 6.7 %collective-permute-start.41 = (f32[64,128]{1,0:T(8,128)S(1)}, f32[64,128]{1,0:T(8,128)S(1)}, u32[]{:S(2)}, u32[]{:S(2)}) collective-permute-start(f32[64,128]{1,0:T(8,128)S(1)} %shard_map.77.refs_0_), channel_id=1, source_target_pairs={{0,8},{4,12},{8,0},{12,4},{16,24},{20,28},{24,16},{28,20},{1,9},{5... | collective-permute-start | bytes 98312 | tf_op jit(solution)/shard_map/ppermute | solution.py:301
  164.1 14.6 %collective-permute-start.62 = (bf16[32,1280]{1,0:T(8,128)(2,1)S(1)}, bf16[32,1280]{1,0:T(8,128)(2,1)S(1)}, u32[]{:S(2)}, u32[]{:S(2)}) collective-permute-start(bf16[32,1280]{1,0:T(8,128)(2,1)S(1)} %shard_map.79.refs_4_), channel_id=1, source_target_pairs={{0,2},{1,3},{2,0},{3,1},{4,6},{5,7},{6,4},{7,5},{8,10},{9,11},{10,... | collective-permute-start | bytes 245768 | tf_op jit(solution)/shard_map/ppermute | solution.py:301
  167.6 11.1 %collective-permute-start.63 = (bf16[32,1280]{1,0:T(8,128)(2,1)S(1)}, bf16[32,1280]{1,0:T(8,128)(2,1)S(1)}, u32[]{:S(2)}, u32[]{:S(2)}) collective-permute-start(bf16[32,1280]{1,0:T(8,128)(2,1)S(1)} %shard_map.79.refs_4_), channel_id=1, source_target_pairs={{0,3},{1,2},{2,1},{3,0},{4,7},{5,6},{6,5},{7,4},{8,11},{9,10},{10,... | collective-permute-start | bytes 245768 | tf_op jit(solution)/shard_map/ppermute | solution.py:301
  (41 other events, 216.1 us)

commit v2 on v1

v2 whole, which is shorter than its diff:
```python
import functools

import jax
import jax.numpy as jnp
from jax import lax
from jax.experimental import pallas as pl
from jax.experimental.pallas import tpu as pltpu
from jax.sharding import PartitionSpec as P

F32 = jnp.float32
BF16 = jnp.bfloat16
EXT = 128
VMEM = pl.BlockSpec(memory_space=pltpu.VMEM)
SMEM = pl.BlockSpec(memory_space=pltpu.SMEM)
UNROLL = 4
PARAMS = pltpu.CompilerParams(vmem_limit_bytes=8 * 1024 * 1024)
PRODUCT_PARAMS = pltpu.CompilerParams(vmem_limit_bytes=27 * 1024 * 1024)


def lanes_of(columns, rows):
    lane = lax.broadcasted_iota(jnp.int32, (rows, EXT), 1)
    out = jnp.zeros((rows, EXT), F32)
    for number, column in enumerate(columns):
        rest = column
        for term in range(3):
            part = rest.astype(BF16).astype(F32)
            rest = rest - part
            out = jnp.where(lane == 3 * number + term, part, out)
    return out.astype(BF16)


def column_of(ext, number):
    lane = lax.broadcasted_iota(jnp.int32, ext.shape, 1)
    chosen = (lane >= 3 * number) & (lane < 3 * number + 3)
    return jnp.sum(jnp.where(chosen, ext, 0.0), axis=1, keepdims=True)


def both_parts(column, half):
    real, imag = parts_of(column, half)
    return join(real + imag, real + imag)


def parts_of(raw, half):
    rows, width = raw.shape
    split = raw.reshape(rows // (2 * half), 2, half, width)
    return split[:, 0], split[:, 1]


def join(first, second):
    groups, half, width = first.shape
    return jnp.stack([first, second], axis=1).reshape(groups * 2 * half, width)


def tile_coeff(vec, tile, rank, conj, half):
    k = tile.shape[2]
    raw = jnp.dot(vec, jnp.concatenate([tile[0], tile[1]], axis=1), preferred_element_type=F32)
    rr, ri = parts_of(raw[:, :k], half)
    ir, ii = parts_of(raw[:, k:], half)
    if conj:
        real, imag = rr + ii, ri - ir
    else:
        real, imag = rr - ii, ri + ir
    lane = lax.broadcasted_iota(jnp.int32, real.shape, 2)
    real = jnp.where(lane < rank, real, 0.0)
    imag = jnp.where(lane < rank, imag, 0.0)
    if conj:
        left = jnp.concatenate([join(real, imag), join(imag, -real)], axis=1)
    else:
        left = jnp.concatenate([join(real, imag), join(-imag, real)], axis=1)
    return left.astype(BF16)


def expand(left, tile):
    right = jnp.concatenate([tile[0], tile[1]], axis=1)
    return lax.dot_general(left, right, (((1,), (1,)), ((), ())), preferred_element_type=F32)


def adjoint_body(n_col, n_row, stream, place, ranks, u_ref, v_ref, *refs):
    pieces, outs, rest = refs[:n_col], refs[n_col : n_col + n_row], refs[n_col + n_row :]
    tile_rows, tile_cols, _, tile_size, _ = u_ref.shape
    if stream:
        u_far, v_far, (u_ref, v_ref, d_scr, z_scr, sems) = u_ref, v_ref, rest

        def copies(i):
            return (
                pltpu.make_async_copy(u_far.at[i], u_ref.at[i], sems.at[0, i]),
                pltpu.make_async_copy(v_far.at[i], v_ref.at[i], sems.at[1, i]),
            )

        for i in range(tile_rows):
            for copy in copies(i):
                copy.start()
    else:
        d_scr, z_scr = rest
    local = pieces[0].shape[1] - EXT
    width = tile_cols * tile_size
    z_scr[...] = jnp.zeros_like(z_scr)
    for j, piece in enumerate(pieces):
        held = jnp.bitwise_xor(place[0], j)
        if local >= tile_size:
            for w in range(local // tile_size):
                d_scr[held * (local // tile_size) + w] = piece[:, w * tile_size : (w + 1) * tile_size]
        else:
            share = tile_size // local
            d_scr[held // share, :, pl.ds(pl.multiple_of((held % share) * local, local), local)] = piece[:, :local]

    def one_row(i, carry):
        if stream:
            for copy in copies(i):
                copy.wait()
        data = d_scr[i]
        half = data.shape[0] // (2 * n_row)
        lefts = [tile_coeff(data, u_ref[i, p], ranks[i, p], True, half) for p in range(tile_cols)]
        for p in range(tile_cols):
            z_scr[:, p * tile_size : (p + 1) * tile_size] += expand(lefts[p], v_ref[i, p])
        return carry

    lax.fori_loop(0, tile_rows, one_row, 0, unroll=1 if stream else UNROLL)
    ext = sum(piece[:, local:].astype(F32) for piece in pieces)
    ext = lanes_of([column_of(ext, 0)], ext.shape[0])
    for k, out in enumerate(outs):
        rows = out.shape[0]
        out[:, :width] = z_scr[k * rows : (k + 1) * rows, :].astype(BF16)
        out[:, width:] = ext[k * rows : (k + 1) * rows, :]


def forward_body(n_col, n_row, place, ranks, u_ref, v_ref, *refs):
    pieces, outs, (x_scr, y_scr) = refs[:n_row], refs[n_row : n_row + 2], refs[n_row + 2 :]
    tile_rows, tile_cols, _, tile_size, _ = u_ref.shape
    width = tile_cols * tile_size
    for k, piece in enumerate(pieces):
        rows = piece.shape[0]
        x_scr[k * rows : (k + 1) * rows, :] = piece[...]
    half = x_scr.shape[0] // (2 * n_row)

    def one_row(i, carry):
        lefts = [
            tile_coeff(x_scr[:, p * tile_size : (p + 1) * tile_size], v_ref[i, p], ranks[i, p], False, half)
            for p in range(tile_cols)
        ]
        y_scr[i] = sum(expand(lefts[p], u_ref[i, p]) for p in range(tile_cols)).astype(BF16)
        return carry

    lax.fori_loop(0, tile_rows, one_row, 0, unroll=UNROLL)
    for j in range(n_col):
        out = outs[j % 2].at[j // 2]
        local = out.shape[1] - EXT
        held = jnp.bitwise_xor(place[0], j)
        if local >= tile_size:
            for w in range(local // tile_size):
                out[:, w * tile_size : (w + 1) * tile_size] = y_scr[held * (local // tile_size) + w]
        else:
            share = tile_size // local
            out[:, :local] = y_scr[held // share, :, pl.ds(pl.multiple_of((held % share) * local, local), local)]
        out[:, local:] = x_scr[:, width:]


def product(body, place, ranks, u_factor, v_factor, pieces, out_shapes, scratch, factors=VMEM):
    return pl.pallas_call(
        body,
        in_specs=[SMEM, SMEM, factors, factors] + [VMEM] * len(pieces),
        out_specs=[VMEM] * len(out_shapes),
        out_shape=out_shapes,
        scratch_shapes=scratch,
        compiler_params=PRODUCT_PARAMS,
    )(place, ranks, u_factor, v_factor, *pieces)


def small(body, out_shapes, *args):
    return pl.pallas_call(
        body,
        in_specs=[SMEM if arg.dtype == jnp.int32 else VMEM for arg in args],
        out_specs=[VMEM] * len(out_shapes),
        out_shape=out_shapes,
        compiler_params=PARAMS,
    )(*args)


def total_of(refs, rows, columns):
    return sum(ref[rows, columns].astype(F32) for ref in refs)


def chip_body(keep, other, *outs):
    chips, rows, wide = keep.shape
    local = wide - EXT
    ext = keep[0, :, local:].astype(F32) + other[0, :, local:].astype(F32)
    ext = lanes_of([column_of(ext, 0), column_of(ext, 1)], rows)
    for k, out in enumerate(outs):
        out[:, :local] = (keep[k, :, :local].astype(F32) + other[k, :, :local].astype(F32)).astype(BF16)
        out[:, local:] = ext


def begin_body(n_row, place, rhs, data, payload):
    rows, local = data.shape
    half = rows // (2 * n_row)
    for k in range(n_row):
        held = jnp.bitwise_xor(place[1], k)
        for part in range(2):
            at = (2 * k + part) * half
            data[at : at + half, :] = rhs[part, pl.ds(pl.multiple_of(held * half, half), half), :]
    values = data[...]
    payload[:, :local] = values.astype(BF16)
    payload[:, local:] = lanes_of([jnp.sum(values * values, axis=1, keepdims=True)], rows)


def model_first_body(n_row, *refs):
    pieces, (v_hat, payload) = refs[:n_row], refs[n_row:]
    width = v_hat.shape[1]
    total = total_of(pieces, slice(None), slice(0, width))
    beta2 = both_parts(column_of(total_of(pieces, slice(None), slice(width, None)), 0), total.shape[0] // 2)
    value = total / jnp.sqrt(beta2)
    v_hat[...] = value
    payload[:, :width] = value.astype(BF16)
    payload[:, width:] = lanes_of([beta2, jnp.sum(value * value, axis=1, keepdims=True)], value.shape[0])


def model_next_body(n_row, v_prev, scalars, *refs):
    pieces, (payload, pair) = refs[:n_row], refs[n_row:]
    rows, width = v_prev.shape
    total = total_of(pieces, slice(None), slice(0, width))
    beta2 = both_parts(column_of(total_of(pieces, slice(None), slice(width, None)), 0), total.shape[0] // 2)
    beta = jnp.sqrt(beta2)
    alpha_prev = scalars[:rows, 0:1]
    value = total / beta - (beta / alpha_prev) * v_prev[...]
    payload[:, :width] = value.astype(BF16)
    payload[:, width:] = lanes_of([beta2, jnp.sum(value * value, axis=1, keepdims=True)], rows)
    pair[:rows, :] = v_prev[...].astype(BF16)
    pair[rows:, :] = value.astype(BF16)


def scalars_of(pieces, local, n_col, n_row):
    ext = total_of(pieces, slice(None), slice(local, None))
    beta = jnp.sqrt(column_of(ext, 0) * (1.0 / n_col))
    alpha = jnp.sqrt(both_parts(column_of(ext, 1), ext.shape[0] // (2 * n_row)))
    return alpha, beta


def data_next_body(n_col, n_row, data_prev, *refs):
    pieces, (data, payload, scalars) = refs[: n_col // 2], refs[n_col // 2 :]
    rows, local = data_prev.shape
    alpha, beta = scalars_of(pieces, local, n_col, n_row)
    value = total_of(pieces, slice(None), slice(0, local)) / alpha - (alpha / beta) * data_prev[...]
    data[...] = value
    payload[:, :local] = value.astype(BF16)
    payload[:, local:] = lanes_of([jnp.sum(value * value, axis=1, keepdims=True)], rows)
    lane = lax.broadcasted_iota(jnp.int32, scalars.shape, 1)
    scalars[...] = jnp.where(lane == 0, alpha, beta)


def data_last_body(n_col, n_row, data_prev, *refs):
    pieces, (square, scalars) = refs[: n_col // 2], refs[n_col // 2 :]
    rows, local = data_prev.shape
    alpha, beta = scalars_of(pieces, local, n_col, n_row)
    value = total_of(pieces, slice(None), slice(0, local)) / alpha - (alpha / beta) * data_prev[...]
    square[...] = jnp.broadcast_to(jnp.sum(value * value, axis=1, keepdims=True), square.shape)
    lane = lax.broadcasted_iota(jnp.int32, scalars.shape, 1)
    scalars[...] = jnp.where(lane == 0, alpha, beta)


def add_body(*refs):
    refs[-1][...] = sum(ref[...] for ref in refs[:-1])


def pick_body(n_col, place, where, *refs):
    pieces, (out, scr) = refs[:n_col], refs[n_col:]
    tile_cols = where.shape[0]
    tile = out.shape[1] // tile_cols
    for j in range(n_col):
        scr[j] = pieces[j][...]
    for p in range(tile_cols):
        held = where[p]
        source = jnp.bitwise_xor(held // tile_cols, place[0])
        at = pl.multiple_of((held % tile_cols) * tile, tile)
        out[:, p * tile : (p + 1) * tile] = scr[source, :, pl.ds(at, tile)]


def finish_body(n_row, place, *refs):
    squares, pieces = refs[:n_row], refs[n_row : 2 * n_row]
    scal_first, scal_next, solution, residual = refs[2 * n_row :]
    rows = squares[0].shape[0]
    total = squares[0][...]
    for k in range(1, n_row):
        other = squares[k][...].reshape(n_row, rows // n_row, squares[k].shape[1])
        moved = jnp.stack([other[g ^ k] for g in range(n_row)], axis=0)
        total = total + moved.reshape(total.shape)
    half = rows // (2 * n_row)
    beta_last = jnp.sqrt(both_parts(total[:, 0:1], half))
    alpha_0, beta_0 = scal_first[:, 0:1], scal_first[:, 1:2]
    alpha_1, beta_1 = scal_next[:, 0:1], scal_next[:, 1:2]
    rho = jnp.sqrt(alpha_0 * alpha_0 + beta_1 * beta_1)
    cosine = alpha_0 / rho
    sine = beta_1 / rho
    theta = sine * alpha_1
    rhobar = -cosine * alpha_1
    phi = cosine * beta_0
    phibar = sine * beta_0
    first = phi / rho
    slope = theta / rho
    rho = jnp.sqrt(rhobar * rhobar + beta_last * beta_last)
    second = (rhobar / rho) * phibar / rho
    phibar = (beta_last / rho) * phibar
    weight_0 = (first - second * slope) / alpha_0
    weight_1 = second / alpha_1
    row = jnp.zeros(residual.shape, F32)
    for k in range(n_row):
        held = jnp.bitwise_xor(place[1], k)
        at = pl.multiple_of(held * half, half)
        lo, hi = 2 * half * k, 2 * half * (k + 1)
        v_0 = pieces[k][: 2 * half, :].astype(F32)
        v_1 = pieces[k][2 * half :, :].astype(F32)
        mixed = weight_0[lo:hi] * v_0 + weight_1[lo:hi] * v_1
        for part in range(2):
            solution[part, pl.ds(at, half), :] = mixed[part * half : (part + 1) * half]
        spread = jnp.broadcast_to(phibar[lo : lo + half], (half, residual.shape[1]))
        lane = lax.broadcasted_iota(jnp.int32, spread.shape, 1)
        source = lax.broadcasted_iota(jnp.int32, spread.shape, 0) + at
        row = row + jnp.sum(jnp.where(lane == source, spread, 0.0), axis=0, keepdims=True)
    residual[...] = row


def swap(value, axis, size, mask):
    return lax.ppermute(value, axis, [(j, j ^ mask) for j in range(size)])


def exchange(pieces, axis, size, step):
    got = {k: swap(pieces[k // step], axis, size, k) for k in reversed(range(step, size, step))}
    return [pieces[0]] + [got[k] for k in sorted(got)]


def gather_row(value, size):
    return exchange([value] * size, "row", size, 1)


def gather_col(value, size):
    pieces = []
    for even in exchange([value] * size, "col", size, 2):
        pieces += [even, swap(even, "col", size, 1)]
    return pieces


def on_device(rhs, u_factor, v_factor, ranks, assign):
    n_col, n_row = lax.axis_size("col"), lax.axis_size("row")
    tile_rows, tile_cols, _, tile_size, _ = u_factor.shape
    sources, local = rhs.shape[1], rhs.shape[3]
    rows = 2 * sources
    share = rows // n_row
    width = tile_cols * tile_size
    place = jnp.stack([lax.axis_index("col"), lax.axis_index("row")]).astype(jnp.int32)
    shape = jax.ShapeDtypeStruct
    data_shape, model_shape = shape((rows, local + EXT), BF16), shape((share, width + EXT), BF16)
    chip_shape, pair_shape = shape((n_col // 2, rows, local + EXT), BF16), shape((2 * share, width), BF16)
    scalar_shape = shape((rows, EXT), F32)
    adjoint_scratch = [pltpu.VMEM((tile_rows, rows, tile_size), BF16), pltpu.VMEM((rows, width), F32)]
    forward_scratch = [pltpu.VMEM((rows, width + EXT), BF16), pltpu.VMEM((tile_rows, rows, tile_size), BF16)]

    def forward(pieces):
        keep, send = product(
            functools.partial(forward_body, n_col, n_row),
            place, ranks, u_near, v_near, pieces, [chip_shape] * 2, forward_scratch,
        )
        sums = small(chip_body, [data_shape] * (n_col // 2), keep, swap(send, "col", n_col, 1))
        return exchange(sums, "col", n_col, 2)

    with jax.named_scope("begin"):
        data_0, payload = small(
            functools.partial(begin_body, n_row),
            [shape((rows, local), F32), data_shape],
            place,
            rhs.reshape(2, sources, local),
        )
        pieces = gather_col(payload, n_col)
    with jax.named_scope("adjoint0"):
        *partial_model, u_near, v_near = product(
            functools.partial(adjoint_body, n_col, n_row, True),
            place, ranks, u_factor, v_factor, pieces,
            [model_shape] * n_row + [shape(u_factor.shape, BF16), shape(v_factor.shape, BF16)],
            adjoint_scratch + [pltpu.SemaphoreType.DMA((2, tile_rows))],
            pl.BlockSpec(memory_space=pl.ANY),
        )
        v_hat_0, model_0 = small(
            functools.partial(model_first_body, n_row),
            [shape((share, width), F32), model_shape],
            *exchange(partial_model, "row", n_row, 1),
        )
        pieces = gather_row(model_0, n_row)
    with jax.named_scope("forward0"):
        data_1, payload, scal_first = small(
            functools.partial(data_next_body, n_col, n_row),
            [shape((rows, local), F32), data_shape, scalar_shape],
            data_0,
            *forward(pieces),
        )
        pieces = gather_col(payload, n_col)
    with jax.named_scope("adjoint1"):
        partial_model = product(
            functools.partial(adjoint_body, n_col, n_row, False),
            place, ranks, u_near, v_near, pieces, [model_shape] * n_row, adjoint_scratch,
        )
        model_1, pair = small(
            functools.partial(model_next_body, n_row),
            [model_shape, pair_shape],
            v_hat_0,
            scal_first,
            *exchange(partial_model, "row", n_row, 1),
        )
        pieces = gather_row(model_1, n_row)
    with jax.named_scope("forward1"):
        chip_sums = forward(pieces)

    with jax.named_scope("natural"):
        natural = lax.axis_index("col") * tile_cols + jnp.arange(tile_cols, dtype=jnp.int32)
        positions = jnp.arange(assign.shape[0], dtype=jnp.int32)
        where_held = jnp.sum(
            positions[None, :] * (assign[None, :] == natural[:, None]).astype(jnp.int32), axis=1
        )
        picked = pl.pallas_call(
            functools.partial(pick_body, n_col),
            in_specs=[SMEM, SMEM] + [VMEM] * n_col,
            out_specs=VMEM,
            out_shape=pair_shape,
            scratch_shapes=[pltpu.VMEM((n_col, 2 * share, width), BF16)],
            compiler_params=PARAMS,
        )(place, where_held, *gather_col(pair, n_col))
        blocks = gather_row(picked, n_row)

    with jax.named_scope("last"):
        square, scal_next = small(
            functools.partial(data_last_body, n_col, n_row),
            [scalar_shape, scalar_shape],
            data_1,
            *chip_sums,
        )
        (square,) = small(add_body, [scalar_shape], square, swap(square, "col", n_col, 1))
        (square,) = small(
            add_body, [scalar_shape], *exchange([square] * n_col, "col", n_col, 2)
        )
        solution, residual = small(
            functools.partial(finish_body, n_row),
            [shape((2, sources, width), F32), shape((1, sources), F32)],
            place,
            *gather_row(square, n_row),
            *blocks,
            scal_first,
            scal_next,
        )
    return (solution, residual.reshape(sources))


def solution(mesh):
    in_specs = (
        P(None, None, "row", "col"),
        P("row", "col", None, None, None),
        P("row", "col", None, None, None),
        P("row", "col"),
        P(),
    )
    out_specs = (P(None, None, "col"), P())
    return jax.shard_map(
        on_device, mesh=mesh, in_specs=in_specs, out_specs=out_specs, check_vma=False
    )
```

time: 187 us -> 123 us (0.66)
  Pallas kernels: 73.3 us -> 31.6 us
  waiting for transfers between devices: 51.5 us -> 40.4 us
  starting transfers between devices: 57.6 us -> 48.6 us
    pallas_call x4, Pallas kernels: 69.3 us -> 27.3 us  [product(): pl.pallas_call(body, in_specs=[SMEM, SMEM, factors, factors] + [VMEM] * l...]
    ppermute x64 -> x51, waiting for transfers between devices: 51.5 us -> 40.4 us  [swap(): return lax.ppermute(value, axis, [(j, j ^ mask) for j in range(size)])]
    ppermute x64 -> x51, starting transfers between devices: 57.6 us -> 48.6 us  [swap(): return lax.ppermute(value, axis, [(j, j ^ mask) for j in range(size)])]
  transfers between devices with their start and end apart: 64 -> 51, of which waited for: 31 -> 31; matrix products, arithmetic and copies ran while one was open for 1% -> 1% of each run, Pallas kernels for 10% -> 1%
where the time goes in v2:
time: 123 us
  starting transfers between devices  48.6 us (40%)
  waiting for transfers between devices  40.4 us (33%)
  Pallas kernels  31.6 us (26%)
  local copies, waits for them, and re-layouts  1.68 us (1%)
    ppermute x51, starting transfers between devices, swap(): return lax.ppermute(value, axis, [(j, j ^ mask) for j in range(size)])  48.6 us
    ppermute x51, waiting for transfers between devices, swap(): return lax.ppermute(value, axis, [(j, j ^ mask) for j in range(size)])  40.4 us
    pallas_call x4, Pallas kernels, product(): pl.pallas_call(body, in_specs=[SMEM, SMEM, factors, factors] + [VMEM] * l...  27.3 us
    pallas_call x10, Pallas kernels, small(): pl.pallas_call(body, in_specs=[SMEM if arg.dtype == jnp.int32 else VMEM f...  3.64 us
  transfers between devices with their start and end apart: 51, of which 31 were waited for; matrix products, arithmetic and copies ran while one was open for 1% of the time, Pallas kernels for 1%

profile of v2, /device:TPU:0, one launch (start us, length us, event | category | flops | bytes accessed | tf_op | source)
XLA Modules:
  0.0 123.3 jit_solution(14942454845767180301)
XLA Ops:
  2.3 4.0 %collective-permute-start.5 = (bf16[64,640]{1,0:T(8,128)(2,1)S(1)}, bf16[64,640]{1,0:T(8,128)(2,1)S(1)}, u32[]{:S(2)}, u32[]{:S(2)}) collective-permute-start(bf16[64,640]{1,0:T(8,128)(2,1)S(1)} %get-tuple-element.38.refs_0_), channel_id=1, source_target_pairs={{0,24},{4,28},{8,16},{12,20},{16,8},{20,12},{24,0},{28,4},{1,25},{... | collective-permute-start | bytes 245768 | tf_op jit(solution)/shard_map/begin/ppermute | solution.py:322
  6.9 1.9 %collective-permute-done.5.refs_6_ = bf16[64,640]{1,0:T(8,128)(2,1)S(1)} collective-permute-done((bf16[64,640]{1,0:T(8,128)(2,1)S(1)}, bf16[64,640]{1,0:T(8,128)(2,1)S(1)}, u32[]{:S(2)}, u32[]{:S(2)}) %collective-permute-start.5) | collective-permute-done | bytes 81952 | tf_op jit(solution)/shard_map/begin/ppermute | solution.py:322
  8.8 1.9 %collective-permute-done.3.refs_4_ = bf16[64,640]{1,0:T(8,128)(2,1)S(1)} collective-permute-done((bf16[64,640]{1,0:T(8,128)(2,1)S(1)}, bf16[64,640]{1,0:T(8,128)(2,1)S(1)}, u32[]{:S(2)}, u32[]{:S(2)}) %collective-permute-start.3) | collective-permute-done | bytes 81952 | tf_op jit(solution)/shard_map/begin/ppermute | solution.py:322
  12.5 9.5 %adjoint0.2 = (bf16[16,1408]{1,0:T(8,128)(2,1)S(1)}, bf16[16,1408]{1,0:T(8,128)(2,1)S(1)}, bf16[16,1408]{1,0:T(8,128)(2,1)S(1)}, bf16[16,1408]{1,0:T(8,128)(2,1)...) custom-call(s32[2]{0:T(128)S(1)} %pad_add_fusion.place, ...), custom_call_target="tpu_custom_call" | custom-call | tf_op jit(solution)/shard_map/adjoint0/pallas_call | solution.py:159
  22.0 1.6 %collective-permute-start.7 = (bf16[16,1408]{1,0:T(8,128)(2,1)S(1)}, bf16[16,1408]{1,0:T(8,128)(2,1)S(1)}, u32[]{:S(2)}, u32[]{:S(2)}) collective-permute-start(bf16[16,1408]{1,0:T(8,128)(2,1)S(1)} %get-tuple-element.42), channel_id=1, source_target_pairs={{0,1},{1,0},{2,3},{3,2},{4,5},{5,4},{6,7},{7,6},{8,9},{9,8},{10,11... | collective-permute-start | bytes 135176 | tf_op jit(solution)/shard_map/adjoint0/ppermute | solution.py:322
  23.6 2.6 %collective-permute-start.8 = (bf16[16,1408]{1,0:T(8,128)(2,1)S(1)}, bf16[16,1408]{1,0:T(8,128)(2,1)S(1)}, u32[]{:S(2)}, u32[]{:S(2)}) collective-permute-start(bf16[16,1408]{1,0:T(8,128)(2,1)S(1)} %get-tuple-element.43), channel_id=1, source_target_pairs={{0,2},{1,3},{2,0},{3,1},{4,6},{5,7},{6,4},{7,5},{8,10},{9,11},{10,... | collective-permute-start | bytes 135176 | tf_op jit(solution)/shard_map/adjoint0/ppermute | solution.py:322
  26.4 2.9 %collective-permute-done.8.refs_2_ = bf16[16,1408]{1,0:T(8,128)(2,1)S(1)} collective-permute-done((bf16[16,1408]{1,0:T(8,128)(2,1)S(1)}, bf16[16,1408]{1,0:T(8,128)(2,1)S(1)}, u32[]{:S(2)}, u32[]{:S(2)}) %collective-permute-start.8) | collective-permute-done | bytes 45088 | tf_op jit(solution)/shard_map/adjoint0/ppermute | solution.py:322
  29.3 2.8 %collective-permute-done.9.refs_3_ = bf16[16,1408]{1,0:T(8,128)(2,1)S(1)} collective-permute-done((bf16[16,1408]{1,0:T(8,128)(2,1)S(1)}, bf16[16,1408]{1,0:T(8,128)(2,1)S(1)}, u32[]{:S(2)}, u32[]{:S(2)}) %collective-permute-start.9) | collective-permute-done | bytes 45088 | tf_op jit(solution)/shard_map/adjoint0/ppermute | solution.py:322
  33.2 3.5 %collective-permute-start.10 = (bf16[16,1408]{1,0:T(8,128)(2,1)S(1)}, bf16[16,1408]{1,0:T(8,128)(2,1)S(1)}, u32[]{:S(2)}, u32[]{:S(2)}) collective-permute-start(bf16[16,1408]{1,0:T(8,128)(2,1)S(1)} %get-tuple-element.45.refs_0_), channel_id=1, source_target_pairs={{0,1},{1,0},{2,3},{3,2},{4,5},{5,4},{6,7},{7,6},{8,9},{9,8},{10,11... | collective-permute-start | bytes 135176 | tf_op jit(solution)/shard_map/adjoint0/ppermute | solution.py:322
  39.2 5.9 %forward0.3 = (bf16[4,64,640]{2,1,0:T(8,128)(2,1)S(1)}, bf16[4,64,640]{2,1,0:T(8,128)(2,1)S(1)}) custom-call(s32[2]{0:T(128)S(1)} %pad_add_fusion.place, s32[16,5]{1,0:T(8,128)S(1)} %copy.12.ranks, bf16[16,5,2,256,128]{4,3,2,1,0:T(8,128)(2,1)S(1)} %get-tuple-element.39.u_ref, bf16[16,5,2,256,128]{4,3,2,1,0:T(8,128)(2,1)S(1)} %get-tuple-element.40.v_ref, ...), custom_call_target="tpu_custom_call" | custom-call | tf_op jit(solution)/shard_map/forward0/pallas_call | solution.py:159
  51.4 1.9 %collective-permute-done.15.refs_2_ = bf16[64,640]{1,0:T(8,128)(2,1)S(1)} collective-permute-done((bf16[64,640]{1,0:T(8,128)(2,1)S(1)}, bf16[64,640]{1,0:T(8,128)(2,1)S(1)}, u32[]{:S(2)}, u32[]{:S(2)}) %collective-permute-start.15) | collective-permute-done | bytes 81952 | tf_op jit(solution)/shard_map/forward0/ppermute | solution.py:322
  54.6 1.8 %collective-permute-start.22 = (bf16[64,640]{1,0:T(8,128)(2,1)S(1)}, bf16[64,640]{1,0:T(8,128)(2,1)S(1)}, u32[]{:S(2)}, u32[]{:S(2)}) collective-permute-start(bf16[64,640]{1,0:T(8,128)(2,1)S(1)} %get-tuple-element.55.refs_0_), channel_id=1, source_target_pairs={{0,24},{4,28},{8,16},{12,20},{16,8},{20,12},{24,0},{28,4},{1,25},{... | collective-permute-start | bytes 245768 | tf_op jit(solution)/shard_map/forward0/ppermute | solution.py:322
  58.2 1.8 %collective-permute-done.22.refs_6_ = bf16[64,640]{1,0:T(8,128)(2,1)S(1)} collective-permute-done((bf16[64,640]{1,0:T(8,128)(2,1)S(1)}, bf16[64,640]{1,0:T(8,128)(2,1)S(1)}, u32[]{:S(2)}, u32[]{:S(2)}) %collective-permute-start.22) | collective-permute-done | bytes 81952 | tf_op jit(solution)/shard_map/forward0/ppermute | solution.py:322
  63.3 6.1 %adjoint1.2 = (bf16[16,1408]{1,0:T(8,128)(2,1)S(1)}, bf16[16,1408]{1,0:T(8,128)(2,1)S(1)}, bf16[16,1408]{1,0:T(8,128)(2,1)S(1)}, bf16[16,1408]{1,0:T(8,128)(2,1)S(1)}) custom-call(s32[2]{0:T(128)S(1)} %pad_add_fusion.place, s32[16,5]{1,0:T(8,128)S(1)} %copy.12.ranks, bf16[16,5,2,256,128]{4,3,2,1,0:T(8,128)(2,1)S(1)} %get-tuple-element.39.u_ref, ...), custom_call_target="tpu_custom_call" | custom-call | tf_op jit(solution)/shard_map/adjoint1/pallas_call | solution.py:159
  69.4 1.7 %collective-permute-start.24 = (bf16[16,1408]{1,0:T(8,128)(2,1)S(1)}, bf16[16,1408]{1,0:T(8,128)(2,1)S(1)}, u32[]{:S(2)}, u32[]{:S(2)}) collective-permute-start(bf16[16,1408]{1,0:T(8,128)(2,1)S(1)} %get-tuple-element.57), channel_id=1, source_target_pairs={{0,1},{1,0},{2,3},{3,2},{4,5},{5,4},{6,7},{7,6},{8,9},{9,8},{10,11... | collective-permute-start | bytes 135176 | tf_op jit(solution)/shard_map/adjoint1/ppermute | solution.py:322
  72.1 1.8 %collective-permute-start.26 = (bf16[16,1408]{1,0:T(8,128)(2,1)S(1)}, bf16[16,1408]{1,0:T(8,128)(2,1)S(1)}, u32[]{:S(2)}, u32[]{:S(2)}) collective-permute-start(bf16[16,1408]{1,0:T(8,128)(2,1)S(1)} %get-tuple-element.59), channel_id=1, source_target_pairs={{0,3},{1,2},{2,1},{3,0},{4,7},{5,6},{6,5},{7,4},{8,11},{9,10},{10,... | collective-permute-start | bytes 135176 | tf_op jit(solution)/shard_map/adjoint1/ppermute | solution.py:322
  73.9 3.3 %collective-permute-done.25.refs_2_ = bf16[16,1408]{1,0:T(8,128)(2,1)S(1)} collective-permute-done((bf16[16,1408]{1,0:T(8,128)(2,1)S(1)}, bf16[16,1408]{1,0:T(8,128)(2,1)S(1)}, u32[]{:S(2)}, u32[]{:S(2)}) %collective-permute-start.25) | collective-permute-done | bytes 45088 | tf_op jit(solution)/shard_map/adjoint1/ppermute | solution.py:322
  78.3 1.8 %collective-permute-start.29 = (bf16[16,1408]{1,0:T(8,128)(2,1)S(1)}, bf16[16,1408]{1,0:T(8,128)(2,1)S(1)}, u32[]{:S(2)}, u32[]{:S(2)}) collective-permute-start(bf16[16,1408]{1,0:T(8,128)(2,1)S(1)} %get-tuple-element.60.refs_0_), channel_id=1, source_target_pairs={{0,3},{1,2},{2,1},{3,0},{4,7},{5,6},{6,5},{7,4},{8,11},{9,10},{10,... | collective-permute-start | bytes 135176 | tf_op jit(solution)/shard_map/adjoint1/ppermute | solution.py:322
  80.5 2.2 %collective-permute-start.27 = (bf16[16,1408]{1,0:T(8,128)(2,1)S(1)}, bf16[16,1408]{1,0:T(8,128)(2,1)S(1)}, u32[]{:S(2)}, u32[]{:S(2)}) collective-permute-start(bf16[16,1408]{1,0:T(8,128)(2,1)S(1)} %get-tuple-element.60.refs_0_), channel_id=1, source_target_pairs={{0,1},{1,0},{2,3},{3,2},{4,5},{5,4},{6,7},{7,6},{8,9},{9,8},{10,11... | collective-permute-start | bytes 135176 | tf_op jit(solution)/shard_map/adjoint1/ppermute | solution.py:322
  85.2 5.9 %forward1.2 = (bf16[4,64,640]{2,1,0:T(8,128)(2,1)S(1)}, bf16[4,64,640]{2,1,0:T(8,128)(2,1)S(1)}) custom-call(s32[2]{0:T(128)S(1)} %pad_add_fusion.place, s32[16,5]{1,0:T(8,128)S(1)} %copy.12.ranks, bf16[16,5,2,256,128]{4,3,2,1,0:T(8,128)(2,1)S(1)} %get-tuple-element.39.u_ref, bf16[16,5,2,256,128]{4,3,2,1,0:T(8,128)(2,1)S(1)} %get-tuple-element.40.v_ref, ...), custom_call_target="tpu_custom_call" | custom-call | tf_op jit(solution)/shard_map/forward1/pallas_call | solution.py:159
  100.9 2.0 %collective-permute-done.33.refs_3_ = bf16[64,640]{1,0:T(8,128)(2,1)S(1)} collective-permute-done((bf16[64,640]{1,0:T(8,128)(2,1)S(1)}, bf16[64,640]{1,0:T(8,128)(2,1)S(1)}, u32[]{:S(2)}, u32[]{:S(2)}) %collective-permute-start.33) | collective-permute-done | bytes 81952 | tf_op jit(solution)/shard_map/forward1/ppermute | solution.py:322
  104.0 1.9 %collective-permute-start.50 = (bf16[32,1280]{1,0:T(8,128)(2,1)S(1)}, bf16[32,1280]{1,0:T(8,128)(2,1)S(1)}, u32[]{:S(2)}, u32[]{:S(2)}) collective-permute-start(bf16[32,1280]{1,0:T(8,128)(2,1)S(1)} %natural.1.refs_4_), channel_id=1, source_target_pairs={{0,3},{1,2},{2,1},{3,0},{4,7},{5,6},{6,5},{7,4},{8,11},{9,10},{10,... | collective-permute-start | bytes 245768 | tf_op jit(solution)/shard_map/natural/ppermute | solution.py:322
  114.8 2.0 %collective-permute-start.40 = (f32[64,128]{1,0:T(8,128)S(1)}, f32[64,128]{1,0:T(8,128)S(1)}, u32[]{:S(2)}, u32[]{:S(2)}) collective-permute-start(f32[64,128]{1,0:T(8,128)S(1)} %last.6.refs_0_), channel_id=1, source_target_pairs={{0,3},{1,2},{2,1},{3,0},{4,7},{5,6},{6,5},{7,4},{8,11},{9,10},{10,... | collective-permute-start | bytes 98312 | tf_op jit(solution)/shard_map/last/ppermute | solution.py:322
  116.8 2.4 %collective-permute-start.38 = (f32[64,128]{1,0:T(8,128)S(1)}, f32[64,128]{1,0:T(8,128)S(1)}, u32[]{:S(2)}, u32[]{:S(2)}) collective-permute-start(f32[64,128]{1,0:T(8,128)S(1)} %last.6.refs_0_), channel_id=1, source_target_pairs={{0,1},{1,0},{2,3},{3,2},{4,5},{5,4},{6,7},{7,6},{8,9},{9,8},{10,11... | collective-permute-start | bytes 98312 | tf_op jit(solution)/shard_map/last/ppermute | solution.py:322
  (100 shorter events, 49.2 us)
Async XLA Ops:
  2.3 6.6 %collective-permute-start.5 = (bf16[64,640]{1,0:T(8,128)(2,1)S(1)}, bf16[64,640]{1,0:T(8,128)(2,1)S(1)}, u32[]{:S(2)}, u32[]{:S(2)}) collective-permute-start(bf16[64,640]{1,0:T(8,128)(2,1)S(1)} %get-tuple-element.38.refs_0_), channel_id=1, source_target_pairs={{0,24},{4,28},{8,16},{12,20},{16,8},{20,12},{24,0},{28,4},{1,25},{... | collective-permute-start | bytes 245768 | tf_op jit(solution)/shard_map/begin/ppermute | solution.py:322
  6.9 5.1 %collective-permute-start = (bf16[64,640]{1,0:T(8,128)(2,1)S(1)}, bf16[64,640]{1,0:T(8,128)(2,1)S(1)}, u32[]{:S(2)}, u32[]{:S(2)}) collective-permute-start(bf16[64,640]{1,0:T(8,128)(2,1)S(1)} %get-tuple-element.38.refs_0_), channel_id=1, source_target_pairs={{0,4},{4,0},{8,12},{12,8},{16,20},{20,16},{24,28},{28,24},{1,5},{5... | collective-permute-start | bytes 245768 | tf_op jit(solution)/shard_map/begin/ppermute | solution.py:322
  23.6 5.7 %collective-permute-start.8 = (bf16[16,1408]{1,0:T(8,128)(2,1)S(1)}, bf16[16,1408]{1,0:T(8,128)(2,1)S(1)}, u32[]{:S(2)}, u32[]{:S(2)}) collective-permute-start(bf16[16,1408]{1,0:T(8,128)(2,1)S(1)} %get-tuple-element.43), channel_id=1, source_target_pairs={{0,2},{1,3},{2,0},{3,1},{4,6},{5,7},{6,4},{7,5},{8,10},{9,11},{10,... | collective-permute-start | bytes 135176 | tf_op jit(solution)/shard_map/adjoint0/ppermute | solution.py:322
  26.2 5.8 %collective-permute-start.9 = (bf16[16,1408]{1,0:T(8,128)(2,1)S(1)}, bf16[16,1408]{1,0:T(8,128)(2,1)S(1)}, u32[]{:S(2)}, u32[]{:S(2)}) collective-permute-start(bf16[16,1408]{1,0:T(8,128)(2,1)S(1)} %get-tuple-element.44), channel_id=1, source_target_pairs={{0,3},{1,2},{2,1},{3,0},{4,7},{5,6},{6,5},{7,4},{8,11},{9,10},{10,... | collective-permute-start | bytes 135176 | tf_op jit(solution)/shard_map/adjoint0/ppermute | solution.py:322
  32.3 5.9 %collective-permute-start.12 = (bf16[16,1408]{1,0:T(8,128)(2,1)S(1)}, bf16[16,1408]{1,0:T(8,128)(2,1)S(1)}, u32[]{:S(2)}, u32[]{:S(2)}) collective-permute-start(bf16[16,1408]{1,0:T(8,128)(2,1)S(1)} %get-tuple-element.45.refs_0_), channel_id=1, source_target_pairs={{0,3},{1,2},{2,1},{3,0},{4,7},{5,6},{6,5},{7,4},{8,11},{9,10},{10,... | collective-permute-start | bytes 135176 | tf_op jit(solution)/shard_map/adjoint0/ppermute | solution.py:322
  33.2 5.9 %collective-permute-start.11 = (bf16[16,1408]{1,0:T(8,128)(2,1)S(1)}, bf16[16,1408]{1,0:T(8,128)(2,1)S(1)}, u32[]{:S(2)}, u32[]{:S(2)}) collective-permute-start(bf16[16,1408]{1,0:T(8,128)(2,1)S(1)} %get-tuple-element.45.refs_0_), channel_id=1, source_target_pairs={{0,2},{1,3},{2,0},{3,1},{4,6},{5,7},{6,4},{7,5},{8,10},{9,11},{10,... | collective-permute-start | bytes 135176 | tf_op jit(solution)/shard_map/adjoint0/ppermute | solution.py:322
  33.2 5.9 %collective-permute-start.10 = (bf16[16,1408]{1,0:T(8,128)(2,1)S(1)}, bf16[16,1408]{1,0:T(8,128)(2,1)S(1)}, u32[]{:S(2)}, u32[]{:S(2)}) collective-permute-start(bf16[16,1408]{1,0:T(8,128)(2,1)S(1)} %get-tuple-element.45.refs_0_), channel_id=1, source_target_pairs={{0,1},{1,0},{2,3},{3,2},{4,5},{5,4},{6,7},{7,6},{8,9},{9,8},{10,11... | collective-permute-start | bytes 135176 | tf_op jit(solution)/shard_map/adjoint0/ppermute | solution.py:322
  48.0 5.3 %collective-permute-start.15 = (bf16[64,640]{1,0:T(8,128)(2,1)S(1)}, bf16[64,640]{1,0:T(8,128)(2,1)S(1)}, u32[]{:S(2)}, u32[]{:S(2)}) collective-permute-start(bf16[64,640]{1,0:T(8,128)(2,1)S(1)} %get-tuple-element.50), channel_id=1, source_target_pairs={{0,16},{4,20},{8,24},{12,28},{16,0},{20,4},{24,8},{28,12},{1,17},{... | collective-permute-start | bytes 245768 | tf_op jit(solution)/shard_map/forward0/ppermute | solution.py:322
  49.0 5.3 %collective-permute-start.16 = (bf16[64,640]{1,0:T(8,128)(2,1)S(1)}, bf16[64,640]{1,0:T(8,128)(2,1)S(1)}, u32[]{:S(2)}, u32[]{:S(2)}) collective-permute-start(bf16[64,640]{1,0:T(8,128)(2,1)S(1)} %get-tuple-element.51), channel_id=1, source_target_pairs={{0,24},{4,28},{8,16},{12,20},{16,8},{20,12},{24,0},{28,4},{1,25},{... | collective-permute-start | bytes 245768 | tf_op jit(solution)/shard_map/forward0/ppermute | solution.py:322
  54.6 5.4 %collective-permute-start.22 = (bf16[64,640]{1,0:T(8,128)(2,1)S(1)}, bf16[64,640]{1,0:T(8,128)(2,1)S(1)}, u32[]{:S(2)}, u32[]{:S(2)}) collective-permute-start(bf16[64,640]{1,0:T(8,128)(2,1)S(1)} %get-tuple-element.55.refs_0_), channel_id=1, source_target_pairs={{0,24},{4,28},{8,16},{12,20},{16,8},{20,12},{24,0},{28,4},{1,25},{... | collective-permute-start | bytes 245768 | tf_op jit(solution)/shard_map/forward0/ppermute | solution.py:322
  71.2 6.1 %collective-permute-start.25 = (bf16[16,1408]{1,0:T(8,128)(2,1)S(1)}, bf16[16,1408]{1,0:T(8,128)(2,1)S(1)}, u32[]{:S(2)}, u32[]{:S(2)}) collective-permute-start(bf16[16,1408]{1,0:T(8,128)(2,1)S(1)} %get-tuple-element.58), channel_id=1, source_target_pairs={{0,2},{1,3},{2,0},{3,1},{4,6},{5,7},{6,4},{7,5},{8,10},{9,11},{10,... | collective-permute-start | bytes 135176 | tf_op jit(solution)/shard_map/adjoint1/ppermute | solution.py:322
  72.1 5.9 %collective-permute-start.26 = (bf16[16,1408]{1,0:T(8,128)(2,1)S(1)}, bf16[16,1408]{1,0:T(8,128)(2,1)S(1)}, u32[]{:S(2)}, u32[]{:S(2)}) collective-permute-start(bf16[16,1408]{1,0:T(8,128)(2,1)S(1)} %get-tuple-element.59), channel_id=1, source_target_pairs={{0,3},{1,2},{2,1},{3,0},{4,7},{5,6},{6,5},{7,4},{8,11},{9,10},{10,... | collective-permute-start | bytes 135176 | tf_op jit(solution)/shard_map/adjoint1/ppermute | solution.py:322
  78.3 5.9 %collective-permute-start.29 = (bf16[16,1408]{1,0:T(8,128)(2,1)S(1)}, bf16[16,1408]{1,0:T(8,128)(2,1)S(1)}, u32[]{:S(2)}, u32[]{:S(2)}) collective-permute-start(bf16[16,1408]{1,0:T(8,128)(2,1)S(1)} %get-tuple-element.60.refs_0_), channel_id=1, source_target_pairs={{0,3},{1,2},{2,1},{3,0},{4,7},{5,6},{6,5},{7,4},{8,11},{9,10},{10,... | collective-permute-start | bytes 135176 | tf_op jit(solution)/shard_map/adjoint1/ppermute | solution.py:322
  80.0 5.2 %collective-permute-start.28 = (bf16[16,1408]{1,0:T(8,128)(2,1)S(1)}, bf16[16,1408]{1,0:T(8,128)(2,1)S(1)}, u32[]{:S(2)}, u32[]{:S(2)}) collective-permute-start(bf16[16,1408]{1,0:T(8,128)(2,1)S(1)} %get-tuple-element.60.refs_0_), channel_id=1, source_target_pairs={{0,2},{1,3},{2,0},{3,1},{4,6},{5,7},{6,4},{7,5},{8,10},{9,11},{10,... | collective-permute-start | bytes 135176 | tf_op jit(solution)/shard_map/adjoint1/ppermute | solution.py:322
  91.2 6.3 %collective-permute-start.46 = (bf16[32,1280]{1,0:T(8,128)(2,1)S(1)}, bf16[32,1280]{1,0:T(8,128)(2,1)S(1)}, u32[]{:S(2)}, u32[]{:S(2)}) collective-permute-start(bf16[32,1280]{1,0:T(8,128)(2,1)S(1)} %get-tuple-element.68.refs_0_), channel_id=1, source_target_pairs={{0,24},{4,28},{8,16},{12,20},{16,8},{20,12},{24,0},{28,4},{1,25},{... | collective-permute-start | bytes 245768 | tf_op jit(solution)/shard_map/natural/ppermute | solution.py:322
  92.3 6.5 %collective-permute-start.44 = (bf16[32,1280]{1,0:T(8,128)(2,1)S(1)}, bf16[32,1280]{1,0:T(8,128)(2,1)S(1)}, u32[]{:S(2)}, u32[]{:S(2)}) collective-permute-start(bf16[32,1280]{1,0:T(8,128)(2,1)S(1)} %get-tuple-element.68.refs_0_), channel_id=1, source_target_pairs={{0,16},{4,20},{8,24},{12,28},{16,0},{20,4},{24,8},{28,12},{1,17},{... | collective-permute-start | bytes 245768 | tf_op jit(solution)/shard_map/natural/ppermute | solution.py:322
  93.3 5.5 %collective-permute-start.42 = (bf16[32,1280]{1,0:T(8,128)(2,1)S(1)}, bf16[32,1280]{1,0:T(8,128)(2,1)S(1)}, u32[]{:S(2)}, u32[]{:S(2)}) collective-permute-start(bf16[32,1280]{1,0:T(8,128)(2,1)S(1)} %get-tuple-element.68.refs_0_), channel_id=1, source_target_pairs={{0,8},{4,12},{8,0},{12,4},{16,24},{20,28},{24,16},{28,20},{1,9},{5... | collective-permute-start | bytes 245768 | tf_op jit(solution)/shard_map/natural/ppermute | solution.py:322
  94.9 5.5 %collective-permute-start.31 = (bf16[64,640]{1,0:T(8,128)(2,1)S(1)}, bf16[64,640]{1,0:T(8,128)(2,1)S(1)}, u32[]{:S(2)}, u32[]{:S(2)}) collective-permute-start(bf16[64,640]{1,0:T(8,128)(2,1)S(1)} %get-tuple-element.64), channel_id=1, source_target_pairs={{0,8},{4,12},{8,0},{12,4},{16,24},{20,28},{24,16},{28,20},{1,9},{5... | collective-permute-start | bytes 245768 | tf_op jit(solution)/shard_map/forward1/ppermute | solution.py:322
  95.5 5.1 %collective-permute-start.32 = (bf16[64,640]{1,0:T(8,128)(2,1)S(1)}, bf16[64,640]{1,0:T(8,128)(2,1)S(1)}, u32[]{:S(2)}, u32[]{:S(2)}) collective-permute-start(bf16[64,640]{1,0:T(8,128)(2,1)S(1)} %get-tuple-element.65), channel_id=1, source_target_pairs={{0,16},{4,20},{8,24},{12,28},{16,0},{20,4},{24,8},{28,12},{1,17},{... | collective-permute-start | bytes 245768 | tf_op jit(solution)/shard_map/forward1/ppermute | solution.py:322
  97.5 5.3 %collective-permute-start.33 = (bf16[64,640]{1,0:T(8,128)(2,1)S(1)}, bf16[64,640]{1,0:T(8,128)(2,1)S(1)}, u32[]{:S(2)}, u32[]{:S(2)}) collective-permute-start(bf16[64,640]{1,0:T(8,128)(2,1)S(1)} %get-tuple-element.66), channel_id=1, source_target_pairs={{0,24},{4,28},{8,16},{12,20},{16,8},{20,12},{24,0},{28,4},{1,25},{... | collective-permute-start | bytes 245768 | tf_op jit(solution)/shard_map/forward1/ppermute | solution.py:322
  104.0 12.8 %collective-permute-start.50 = (bf16[32,1280]{1,0:T(8,128)(2,1)S(1)}, bf16[32,1280]{1,0:T(8,128)(2,1)S(1)}, u32[]{:S(2)}, u32[]{:S(2)}) collective-permute-start(bf16[32,1280]{1,0:T(8,128)(2,1)S(1)} %natural.1.refs_4_), channel_id=1, source_target_pairs={{0,3},{1,2},{2,1},{3,0},{4,7},{5,6},{6,5},{7,4},{8,11},{9,10},{10,... | collective-permute-start | bytes 245768 | tf_op jit(solution)/shard_map/natural/ppermute | solution.py:322
  107.0 12.3 %collective-permute-start.49 = (bf16[32,1280]{1,0:T(8,128)(2,1)S(1)}, bf16[32,1280]{1,0:T(8,128)(2,1)S(1)}, u32[]{:S(2)}, u32[]{:S(2)}) collective-permute-start(bf16[32,1280]{1,0:T(8,128)(2,1)S(1)} %natural.1.refs_4_), channel_id=1, source_target_pairs={{0,2},{1,3},{2,0},{3,1},{4,6},{5,7},{6,4},{7,5},{8,10},{9,11},{10,... | collective-permute-start | bytes 245768 | tf_op jit(solution)/shard_map/natural/ppermute | solution.py:322
  108.1 11.2 %collective-permute-start.48 = (bf16[32,1280]{1,0:T(8,128)(2,1)S(1)}, bf16[32,1280]{1,0:T(8,128)(2,1)S(1)}, u32[]{:S(2)}, u32[]{:S(2)}) collective-permute-start(bf16[32,1280]{1,0:T(8,128)(2,1)S(1)} %natural.1.refs_4_), channel_id=1, source_target_pairs={{0,1},{1,0},{2,3},{3,2},{4,5},{5,4},{6,7},{7,6},{8,9},{9,8},{10,11... | collective-permute-start | bytes 245768 | tf_op jit(solution)/shard_map/natural/ppermute | solution.py:322
  114.8 5.8 %collective-permute-start.40 = (f32[64,128]{1,0:T(8,128)S(1)}, f32[64,128]{1,0:T(8,128)S(1)}, u32[]{:S(2)}, u32[]{:S(2)}) collective-permute-start(f32[64,128]{1,0:T(8,128)S(1)} %last.6.refs_0_), channel_id=1, source_target_pairs={{0,3},{1,2},{2,1},{3,0},{4,7},{5,6},{6,5},{7,4},{8,11},{9,10},{10,... | collective-permute-start | bytes 98312 | tf_op jit(solution)/shard_map/last/ppermute | solution.py:322
  (28 other events, 120.7 us)
